TPU v7x, 32 devices: a whole 2x2x4 slice. The times are simulated.
32 devices in a mesh: seq: 16 (over z, x, core), tp: 2 (over y).
Axes of the slice: x: 2, y: 2, z: 4, core: 2. Of those that a mesh axis runs over, the one named last changes fastest.
Arguments:
- hidden_in: bfloat16 [2048, 4096], P('seq', 'tp'), may hold values from -64 to 64
- span_order: int32 [16], replicated, may hold values from 0 to 15, each once
- norm_gain: bfloat16 [4096], P('tp'), may hold values from 0.099609375 to 1.8984375
- w_query: bfloat16 [4096, 4096], P('seq', 'tp'), may hold values from -0.09375 to 0.09375
- bias_query: bfloat16 [4096], P('tp'), may hold values from -14 to 14
- key_value_weight: bfloat16 [4096, 2, 1024], P('seq', None, 'tp'), may hold values from -0.09375 to 0.09375
- bias_kv: bfloat16 [2, 1024], P(None, 'tp'), may hold values from -14 to 14
- w_out: bfloat16 [4096, 4096], P('tp', 'seq'), may hold values from -0.09375 to 0.09375
- post_gain: bfloat16 [4096], P('tp'), may hold values from 0.099609375 to 1.8984375
Outputs:
- attn_out: bfloat16 [2048, 4096], P('seq', 'tp')
- normed: bfloat16 [2048, 4096], P('seq', 'tp')
Inputs may be any that keep to these rules, and one draw needn't show every extreme that they name: Each span number appears once; row r of hidden_in belongs to span span_order[r // 128].
All inputs are finite; a program needn't handle non-finite values.
Results may differ from a plain program's by a relative error of at most 0.014.
Values may be sent and summed in bfloat16 or wider, within the bound.
A program may use at most 128 MiB of HBM per device.

v0:
```python
import math

import jax
import jax.numpy as jnp
from jax import lax
from jax.sharding import PartitionSpec as P

MODEL_WIDTH = 4096
HEAD_SIZE = 128
GROUP = 4


eps = 1e-06
rope_base = 1000000.0


def apply_rotary(field, token_positions):
    half = field.shape[-1] // 2
    inverse = jnp.exp(-math.log(rope_base) * jnp.arange(half, dtype=jnp.float32) / half)
    angles = token_positions.astype(jnp.float32)[:, None] * inverse[None, :]
    cosine = jnp.cos(angles)[:, None, :]
    sine = jnp.sin(angles)[:, None, :]
    first = field[..., :half]
    second = field[..., half:]
    return jnp.concatenate(
        [first * cosine - second * sine, second * cosine + first * sine], axis=-1
    )


def span_lookup(order, devices):
    table_ids = jnp.arange(order.shape[0], dtype=jnp.int32)
    return jnp.sum(jnp.where(devices[:, None] == table_ids[None, :], order[None, :], 0), axis=1)


def per_device(
    hidden_in,
    span_order,
    norm_gain,
    w_query,
    bias_query,
    key_value_weight,
    bias_kv,
    w_out,
    post_gain,
):
    tok_rows = hidden_in.shape[0]
    seq_index = lax.axis_index("seq")
    own_span = span_lookup(span_order, jnp.full((1,), seq_index, jnp.int32))[0]
    token_positions = own_span * tok_rows + jnp.arange(tok_rows, dtype=jnp.int32)
    local = hidden_in.astype(jnp.float32)
    raw_rows, gains = (
        lax.all_gather(hidden_in, "tp", axis=1, tiled=True),
        lax.all_gather(norm_gain[None, :], "tp", axis=1, tiled=True),
    )
    full_rows = raw_rows.astype(jnp.float32)
    meansq = jnp.mean(full_rows * full_rows, axis=1, keepdims=True)
    normed_in = (full_rows * lax.rsqrt(meansq + eps) * gains.astype(jnp.float32)).astype(
        jnp.bfloat16
    )
    columns = normed_in
    query_proj = jnp.dot(
        columns,
        lax.all_gather(w_query, "seq", axis=0, tiled=True),
        preferred_element_type=jnp.float32,
    )
    columns = normed_in
    pair_proj = jnp.einsum(
        "tr,rkc->tkc",
        columns,
        lax.all_gather(key_value_weight, "seq", axis=0, tiled=True),
        preferred_element_type=jnp.float32,
    )
    query_heads = w_query.shape[1] // HEAD_SIZE
    kv_heads = key_value_weight.shape[2] // HEAD_SIZE
    query_proj = query_proj + bias_query.astype(jnp.float32)[None, :]
    queries = apply_rotary(
        query_proj.reshape(tok_rows, query_heads, HEAD_SIZE), token_positions
    ).astype(jnp.bfloat16)
    pair_proj = pair_proj + bias_kv.astype(jnp.float32)[None, :, :]
    rotated_keys = apply_rotary(
        pair_proj[:, 0, :].reshape(tok_rows, kv_heads, HEAD_SIZE), token_positions
    )
    rotated_keys = rotated_keys.astype(jnp.bfloat16).reshape(tok_rows, kv_heads * HEAD_SIZE)
    value_rows = pair_proj[:, 1, :].astype(jnp.bfloat16)
    grouped = (
        queries.reshape(tok_rows, kv_heads, GROUP, HEAD_SIZE)
        .transpose(1, 2, 0, 3)
        .reshape(kv_heads, GROUP * tok_rows, HEAD_SIZE)
    )
    query_pos = jnp.tile(token_positions, GROUP)
    last_query = jnp.max(token_positions)
    scale = 1.0 / math.sqrt(HEAD_SIZE)
    start_state = (
        jnp.full((kv_heads, GROUP * tok_rows), -1e30, jnp.float32),
        jnp.zeros((kv_heads, GROUP * tok_rows), jnp.float32),
        jnp.zeros((kv_heads, GROUP * tok_rows, HEAD_SIZE), jnp.float32),
    )
    key_piece = lax.all_gather(rotated_keys, "seq", axis=0, tiled=True)
    value_piece = lax.all_gather(value_rows, "seq", axis=0, tiled=True)
    count = key_piece.shape[0]
    block = math.gcd(count, 1536)

    def visit(step, state):
        first = step * block
        key_block = lax.dynamic_slice_in_dim(key_piece, first, block, 0).reshape(
            block, kv_heads, HEAD_SIZE
        )
        value_block = lax.dynamic_slice_in_dim(value_piece, first, block, 0).reshape(
            block, kv_heads, HEAD_SIZE
        )
        row_ids = first + jnp.arange(block, dtype=jnp.int32)
        key_pos = span_lookup(span_order, row_ids // tok_rows) * tok_rows + row_ids % tok_rows

        def update(current):
            maxima, totals, sums = current
            scores = (
                jnp.einsum("kqd,nkd->kqn", grouped, key_block, preferred_element_type=jnp.float32)
                * scale
            )
            allowed = (key_pos[None, :] <= query_pos[:, None])[None, :, :]
            scores = jnp.where(allowed, scores, -1e30)
            fresh = jnp.maximum(maxima, jnp.max(scores, axis=2))
            weights = jnp.where(allowed, jnp.exp(scores - fresh[:, :, None]), 0.0)
            factor = jnp.exp(maxima - fresh)
            totals = totals * factor + jnp.sum(weights, axis=2)
            sums = sums * factor[:, :, None] + jnp.einsum(
                "kqn,nkd->kqd",
                weights.astype(jnp.bfloat16),
                value_block,
                preferred_element_type=jnp.float32,
            )
            return (fresh, totals, sums)

        return lax.cond(jnp.min(key_pos) <= last_query, update, lambda current: current, state)

    maxima, totals, sums = lax.fori_loop(0, count // block, visit, start_state)
    attended = (sums / totals[:, :, None]).astype(jnp.bfloat16)
    attended = (
        attended.reshape(kv_heads, GROUP, tok_rows, HEAD_SIZE)
        .transpose(2, 0, 1, 3)
        .reshape(tok_rows, query_heads * HEAD_SIZE)
    )
    partial_out = jnp.dot(
        attended,
        lax.all_gather(w_out, "seq", axis=1, tiled=True),
        preferred_element_type=jnp.float32,
    )
    mixed = lax.psum_scatter(
        partial_out.astype(jnp.bfloat16), "tp", scatter_dimension=1, tiled=True
    ).astype(jnp.float32)
    attn_out = mixed.astype(jnp.bfloat16)
    stream = local + mixed
    post_sq = lax.psum(jnp.sum(stream * stream, axis=1), "tp")
    normed = (
        stream
        * lax.rsqrt(post_sq / MODEL_WIDTH + eps)[:, None]
        * post_gain.astype(jnp.float32)[None, :]
    ).astype(jnp.bfloat16)
    return (attn_out, normed)


def solution(mesh):
    placed = (
        P("seq", "tp"),
        P(),
        P("tp"),
        P("seq", "tp"),
        P("tp"),
        P("seq", None, "tp"),
        P(None, "tp"),
        P("tp", "seq"),
        P("tp"),
    )
    return jax.shard_map(
        per_device,
        mesh=mesh,
        in_specs=placed,
        out_specs=(P("seq", "tp"), P("seq", "tp")),
        check_vma=False,
    )
```

profile of v0, /device:TPU:26, one launch (start us, length us, event | category | flops | bytes accessed | tf_op | source)
XLA Modules:
  0.0 497.9 jit_solution(17849845767442077635)
XLA Ops:
  7.2 0.7 all-gather.9.cloned.1.call-update
  7.9 1.9 copy.44
  9.9 4.5 all-gather
  14.4 0.7 convert_element_type.69
  15.1 16.7 %all-gather.9.cloned.1.call-done = bf16[128,4096]{1,0:T(8,128)(2,1)} async-done(((bf16[128,2048]{1,0:T(8,128)(2,1)}), bf16[128,4096]{1,0:T(8,128)(2,1)}) %all-gather.9.cloned.1.call-update) | async-done | bytes 1048592 | tf_op jit(solution)/shard_map/all_gather | solution.py:52
  31.8 1.5 fusion.18
  33.3 73.2 %all-gather.11.cloned.1.call-done = bf16[4096,2,512]{2,0,1:T(8,128)(2,1)} async-done(((bf16[256,2,512]{2,0,1:T(8,128)(2,1)}), bf16[4096,2,512]{2,0,1:T(8,128)(2,1)}) %all-gather.11.cloned.1.call-update) | async-done | bytes 8388624 | tf_op jit(solution)/shard_map/all_gather | solution.py:70
  106.6 5.0 %convolution_add_fusion.1 = f32[128,2,512]{2,0,1:T(8,128)S(1)} fusion(bf16[4096,2,512]{2,0,1:T(8,128)(2,1)} %all-gather.11.cloned.1.call-done, bf16[128,4096]{1,0:T(8,128)(2,1)} %all-gather.9.cloned.1.call-done, f32[4096]{0:T(1024)S(1)} %mul.210, f32[128]{0:T(128)S(1)} %add_rsqrt_fusion.1, f32[2,512]{1,0:T(2,128)S(1)} %convert_element_type.69), kind=kOutput, calls=%fused_computation.39 | convolution fusion | flops 1075970048 | bytes 9982464 | tf_op jit(solution)/shard_map/tr,rkc->tkc/dot_general | solution.py:67
  111.6 0.7 slice.40
  115.2 0.8 copy.45
  117.4 35.2 %all-gather.19.cloned.1.call-done = bf16[2048,1,512]{2,0,1:T(8,128)(2,1)} async-done(((bf16[128,1,512]{2,0,1:T(8,128)(2,1)}), bf16[2048,1,512]{2,0,1:T(8,128)(2,1)}) %all-gather.19.cloned.1.call-update) | async-done | bytes 2097168 | tf_op jit(solution)/shard_map/all_gather | solution.py:99
  152.7 2.9 copy.48
  155.6 123.6 %all-gather.15.cloned.1.call-done = bf16[4096,2048]{1,0:T(8,128)(2,1)} async-done(((bf16[256,2048]{1,0:T(8,128)(2,1)}), bf16[4096,2048]{1,0:T(8,128)(2,1)}) %all-gather.15.cloned.1.call-update) | async-done | bytes 16777232 | tf_op jit(solution)/shard_map/all_gather | solution.py:63
  279.2 8.2 %fusion.21 = f32[16,8,16,128]{3,1,2,0:T(8,128)S(1)} fusion(bf16[4096,2048]{1,0:T(8,128)(2,1)} %all-gather.15.cloned.1.call-done, f32[2048]{0:T(1024)S(1)} %convert_element_type.72, bf16[128,4096]{1,0:T(8,128)(2,1)S(1)} %copy-done, f32[4096]{0:T(1024)S(1)} %mul.210, f32[128]{0:T(128)S(1)} %add_rsqrt_fusion.1), kind=kOutput, calls=%fused_computation.38 | convolution fusion | flops 2149842944 | bytes 18899456 | tf_op jit(solution)/shard_map/dot_general | solution.py:61
  288.7 33.2 %all-gather.13.cloned.1.call-done = bf16[2048,512]{0,1:T(8,128)(2,1)} async-done(((bf16[128,512]{0,1:T(8,128)(2,1)}), bf16[2048,512]{0,1:T(8,128)(2,1)}) %all-gather.13.cloned.1.call-update) | async-done | bytes 2097168 | tf_op jit(solution)/shard_map/all_gather | solution.py:98
  321.9 1.1 broadcast_in_dim.105
  322.9 33.3 %while.20 = (s32[]{:T(128)}, f32[4,512]{1,0:T(4,128)S(1)}, f32[4,512]{1,0:T(4,128)S(1)}, f32[4,512,128]{2,1,0:T(8,128)}, s32[16]{0:T(128)S(1)}, /*index=5*/s32[]...) while((s32[]{:T(128)}, f32[4,512]{1,0:T(4,128)S(1)}, ...), condition=%wide.region_10.11_spmd.clone, body=%wide.region_3.10_spmd.clone.sunk | while | flops 551332864 | bytes 27935672 | solution.py:136
  324.9 6.3 %conditional.3 = ((f32[4,512]{1,0:T(4,128)S(1)}, f32[4,512]{1,0:T(4,128)S(1)}, f32[4,512,128]{2,1,0:T(8,128)})) conditional(s32[]{:T(128)} %convert_element_type.117, (f32[4,512]{1,0:T(4,128)S(1)}, f32[4,512]{1,0:T(4,128)S(1)}, f32[4,512,128]{2,1,0:T(8,128)}) %tuple.77, (s32[512]{0:T(512)S(1)}, s32[128]{0:T(128)S(1)}, s32[]{:T(128)}, ...), branch_computations={%region_6.6_spmd, %region_7.9_spmd} | conditional | flops 551292928 | bytes 27925118 | solution.py:134
  325.0 1.1 constant_dynamic-slice_fusion
  326.3 1.0 fusion.2
  327.4 1.0 fusion.4
  328.5 1.8 fusion.8
  330.3 1.0 copy-done.3
  333.2 6.4 %conditional.3 = ((f32[4,512]{1,0:T(4,128)S(1)}, f32[4,512]{1,0:T(4,128)S(1)}, f32[4,512,128]{2,1,0:T(8,128)})) conditional(s32[]{:T(128)} %convert_element_type.117, (f32[4,512]{1,0:T(4,128)S(1)}, f32[4,512]{1,0:T(4,128)S(1)}, f32[4,512,128]{2,1,0:T(8,128)}) %tuple.77, (s32[512]{0:T(512)S(1)}, s32[128]{0:T(128)S(1)}, s32[]{:T(128)}, ...), branch_computations={%region_6.6_spmd, %region_7.9_spmd} | conditional | flops 551292928 | bytes 27925118 | solution.py:134
  333.3 1.2 constant_dynamic-slice_fusion
  334.7 1.0 fusion.2
  335.8 1.0 fusion.4
  336.8 1.8 fusion.8
  338.6 1.0 copy-done.3
  341.6 6.3 %conditional.3 = ((f32[4,512]{1,0:T(4,128)S(1)}, f32[4,512]{1,0:T(4,128)S(1)}, f32[4,512,128]{2,1,0:T(8,128)})) conditional(s32[]{:T(128)} %convert_element_type.117, (f32[4,512]{1,0:T(4,128)S(1)}, f32[4,512]{1,0:T(4,128)S(1)}, f32[4,512,128]{2,1,0:T(8,128)}) %tuple.77, (s32[512]{0:T(512)S(1)}, s32[128]{0:T(128)S(1)}, s32[]{:T(128)}, ...), branch_computations={%region_6.6_spmd, %region_7.9_spmd} | conditional | flops 551292928 | bytes 27925118 | solution.py:134
  341.7 1.1 constant_dynamic-slice_fusion
  343.0 1.0 fusion.2
  344.1 1.0 fusion.4
  345.1 1.8 fusion.8
  347.0 1.0 copy-done.3
  349.9 6.3 %conditional.3 = ((f32[4,512]{1,0:T(4,128)S(1)}, f32[4,512]{1,0:T(4,128)S(1)}, f32[4,512,128]{2,1,0:T(8,128)})) conditional(s32[]{:T(128)} %convert_element_type.117, (f32[4,512]{1,0:T(4,128)S(1)}, f32[4,512]{1,0:T(4,128)S(1)}, f32[4,512,128]{2,1,0:T(8,128)}) %tuple.77, (s32[512]{0:T(512)S(1)}, s32[128]{0:T(128)S(1)}, s32[]{:T(128)}, ...), branch_computations={%region_6.6_spmd, %region_7.9_spmd} | conditional | flops 551292928 | bytes 27925118 | solution.py:134
  350.0 1.1 constant_dynamic-slice_fusion
  351.4 1.0 fusion.2
  352.4 1.0 fusion.4
  353.5 1.8 fusion.8
  355.3 1.0 copy-done.3
  356.3 1.6 divide_convert_fusion
  358.1 93.9 %all-gather.17.cloned.1.call-done = bf16[2048,4096]{1,0:T(8,128)(2,1)} async-done(((bf16[2048,256]{1,0:T(8,128)(2,1)}), bf16[2048,4096]{1,0:T(8,128)(2,1)}) %all-gather.17.cloned.1.call-update) | async-done | bytes 16777232 | tf_op jit(solution)/shard_map/all_gather | solution.py:145
  452.0 9.2 %convolution_convert_fusion = bf16[128,4096]{1,0:T(8,128)(2,1)} fusion(bf16[128,2048]{0,1:T(8,128)(2,1)S(1)} %bitcast.47, bf16[2048,4096]{1,0:T(8,128)(2,1)} %all-gather.17.cloned.1.call-done), kind=kOutput, calls=%fused_computation.31 | convolution fusion | flops 2148007936 | bytes 18350080 | tf_op jit(solution)/shard_map/dot_general | solution.py:143
  461.3 21.5 %reduce-scatter.2.cloned.1.call-done = bf16[128,2048]{1,0:T(8,128)(2,1)} async-done(((bf16[128,4096]{1,0:T(8,128)(2,1)}), bf16[128,2048]{1,0:T(8,128)(2,1)}) %reduce-scatter.2.cloned.1.call-update) | async-done | bytes 524304 | tf_op jit(solution)/shard_map/reduce_scatter | solution.py:148
  482.8 1.3 multiply_reduce_fusion
  484.1 4.9 psum.7
  489.0 2.0 multiply_convert_fusion
  (89 shorter events, 9.3 us)
Async XLA Ops:
  7.2 24.6 %all-gather.9.cloned.1.call-start = ((), (), s32[]{:S(2)}) async-start(), calls=%async_computation.1 | async-start | bytes 1572864 | tf_op jit(solution)/shard_map/all_gather | solution.py:52
  7.9 98.7 %all-gather.11.cloned.1.call-start = ((), (), s32[]{:S(2)}) async-start(), calls=%async_computation.2 | async-start | bytes 8912896 | tf_op jit(solution)/shard_map/all_gather | solution.py:70
  9.9 142.8 %all-gather.19.cloned.1.call-start = ((), (), s32[]{:S(2)}) async-start(), calls=%async_computation.7 | async-start | bytes 2228224 | tf_op jit(solution)/shard_map/all_gather | solution.py:99
  33.3 79.6 %copy-start.4 = (s32[16]{0:T(128)S(1)}, s32[16]{0:T(128)}, u32[]{:S(2)}) copy-start(s32[16]{0:T(128)} %param.14) | copy-start | bytes 196
  111.6 5.2 %copy-start.5 = (bf16[2048]{0:T(1024)(128)(2,1)S(1)}, bf16[2048]{0:T(1024)(128)(2,1)}, u32[]{:S(2)}) copy-start(bf16[2048]{0:T(1024)(128)(2,1)} %param.17) | copy-start | bytes 12292
  112.3 166.9 %all-gather.15.cloned.1.call-start = ((), (), s32[]{:S(2)}) async-start(), calls=%async_computation.4 | async-start | bytes 17825792 | tf_op jit(solution)/shard_map/all_gather | solution.py:63
  112.9 166.3 %copy-start = (bf16[128,4096]{1,0:T(8,128)(2,1)S(1)}, bf16[128,4096]{1,0:T(8,128)(2,1)}, u32[]{:S(2)}) copy-start(bf16[128,4096]{1,0:T(8,128)(2,1)} %all-gather.9.cloned.1.call-done) | copy-start | bytes 3145732
  112.9 209.0 %all-gather.13.cloned.1.call-start = ((), (), s32[]{:S(2)}) async-start(), calls=%async_computation.3 | async-start | bytes 2228224 | tf_op jit(solution)/shard_map/all_gather | solution.py:98
  116.0 336.1 %all-gather.17.cloned.1.call-start = ((), (), s32[]{:S(2)}) async-start(), calls=%async_computation.5 | async-start | bytes 17825792 | tf_op jit(solution)/shard_map/all_gather | solution.py:145
  116.6 366.2 %reduce-scatter.2.cloned.1.call-start = ((), (), s32[]{:S(2)}) async-start(), calls=%async_computation.6 | async-start | bytes 1572864 | tf_op jit(solution)/shard_map/reduce_scatter | solution.py:148
  326.3 2.1 copy-start.2
  330.2 1.0 copy-start.3
  334.7 2.1 copy-start.2
  338.6 1.0 copy-start.3
  343.0 2.1 copy-start.2
  346.9 1.0 copy-start.3
  351.3 2.1 copy-start.2
  355.3 1.0 copy-start.3
  452.0 9.2 %copy-start.6 = (bf16[2048]{0:T(1024)(128)(2,1)S(1)}, bf16[2048]{0:T(1024)(128)(2,1)}, u32[]{:S(2)}) copy-start(bf16[2048]{0:T(1024)(128)(2,1)} %param.21) | copy-start | bytes 12292
  452.0 30.7 %copy-start.1 = (bf16[128,2048]{1,0:T(8,128)(2,1)S(1)}, bf16[128,2048]{1,0:T(8,128)(2,1)}, u32[]{:S(2)}) copy-start(bf16[128,2048]{1,0:T(8,128)(2,1)} %param.13) | copy-start | bytes 1572868
Sparse Core Ops, SparseCore 0:
  9.5 22.2 all-gather.8
  34.5 71.9 all-gather.10
  112.4 40.1 all-gather.18
  154.7 124.4 all-gather.14
  281.7 40.0 all-gather.12
  323.9 128.1 all-gather.16
  461.4 21.3 reduce-scatter.1
where the time goes:
time: 500 us; the launch traced here: 498 us
  waiting for transfers between devices  399 us (80%)
  matrix products  33.5 us (7%)
  other arithmetic  18.1 us (4%)
  local copies, waits for them, and re-layouts  16.8 us (3%)
  between operations  15 us (3%)
  blocking collectives  9.42 us (2%)
  loops' own time  5.47 us (1%)
    all_gather x1, waiting for transfers between devices, per_device(): lax.all_gather(w_query, 'seq', axis=0, tiled=True)  124 us
    all_gather x1, waiting for transfers between devices, per_device(): lax.all_gather(w_out, 'seq', axis=1, tiled=True)  93.9 us
    all_gather x1, waiting for transfers between devices, per_device(): lax.all_gather(key_value_weight, 'seq', axis=0, tiled=True)  73.2 us
    all_gather x1, waiting for transfers between devices, per_device(): value_piece = lax.all_gather(value_rows, 'seq', axis=0, tiled=True)  35.2 us
    all_gather x1, waiting for transfers between devices, per_device(): key_piece = lax.all_gather(rotated_keys, 'seq', axis=0, tiled=True)  33.2 us
    reduce_scatter x1, waiting for transfers between devices, per_device(): lax.psum_scatter(partial_out.astype(jnp.bfloat16), 'tp', scatter_dimensio...  21.5 us
    all_gather x1, waiting for transfers between devices, per_device(): lax.all_gather(hidden_in, 'tp', axis=1, tiled=True)  16.7 us
  transfers between devices with their start and end apart: 7, of which 7 were waited for; matrix products, arithmetic and copies ran while one was open for 9% of the time, Pallas kernels for 0%

commit v1 on v0

--- a/solution.py
+++ b/solution.py
@@ -3,6 +3,8 @@
 import jax
 import jax.numpy as jnp
 from jax import lax
+from jax.experimental import pallas as pl
+from jax.experimental.pallas import tpu as pltpu
 from jax.sharding import PartitionSpec as P
 
 MODEL_WIDTH = 4096
@@ -32,7 +34,7 @@
     return jnp.sum(jnp.where(devices[:, None] == table_ids[None, :], order[None, :], 0), axis=1)
 
 
-def per_device(
+def per_device_by_span(
     hidden_in,
     span_order,
     norm_gain,
@@ -159,6 +161,149 @@
     return (attn_out, normed)
 
 
+def rope_tables(span_order, tok_rows):
+    half = HEAD_SIZE // 2
+    rows = (span_order[:, None] * tok_rows + jnp.arange(tok_rows, dtype=jnp.int32)[None, :]).reshape(-1)
+    inverse = jnp.exp(-math.log(rope_base) * jnp.arange(half, dtype=jnp.float32) / half)
+    angles = rows.astype(jnp.float32)[:, None] * inverse[None, :]
+    cosine, sine = jnp.cos(angles), jnp.sin(angles)
+    return (
+        rows,
+        jnp.concatenate([cosine, cosine], axis=1),
+        jnp.concatenate([-sine, sine], axis=1),
+    )
+
+
+def attention_kernel(q_ref, k_ref, v_ref, qpos_ref, kpos_ref, out_ref):
+    scores = lax.dot_general(
+        q_ref[...], k_ref[...], (((1,), (1,)), ((), ())), preferred_element_type=jnp.float32
+    ) * (1.0 / math.sqrt(HEAD_SIZE))
+    allowed = kpos_ref[...] <= qpos_ref[...]
+    scores = jnp.where(allowed, scores, -jnp.inf)
+    peak = jnp.max(scores, axis=1, keepdims=True)
+    weights = jnp.exp(scores - peak)
+    totals = jnp.sum(weights, axis=1, keepdims=True)
+    summed = jnp.dot(
+        weights.astype(jnp.bfloat16), v_ref[...], preferred_element_type=jnp.float32
+    )
+    out_ref[...] = (summed / totals).astype(jnp.bfloat16)
+
+
+def attention(queries, keys, values, positions):
+    count = queries.shape[0]
+    block = math.gcd(count, 256)
+    rows = pl.BlockSpec((block, HEAD_SIZE), lambda i: (i, 0))
+    whole = pl.BlockSpec((count, HEAD_SIZE), lambda i: (0, 0))
+    return pl.pallas_call(
+        attention_kernel,
+        grid=(count // block,),
+        in_specs=[
+            rows,
+            whole,
+            whole,
+            pl.BlockSpec((block, 1), lambda i: (i, 0)),
+            pl.BlockSpec((1, count), lambda i: (0, 0)),
+        ],
+        out_specs=rows,
+        out_shape=jax.ShapeDtypeStruct((count, HEAD_SIZE), jnp.bfloat16),
+        cost_estimate=pl.CostEstimate(
+            flops=4 * count * count * HEAD_SIZE,
+            bytes_accessed=8 * count * HEAD_SIZE,
+            transcendentals=count * count,
+        ),
+        name="attention",
+    )(queries, keys, values, positions[:, None], positions[None, :])
+
+
+def per_device_by_head(
+    hidden_in,
+    span_order,
+    norm_gain,
+    w_query,
+    bias_query,
+    key_value_weight,
+    bias_kv,
+    w_out,
+    post_gain,
+):
+    tok_rows, width = hidden_in.shape
+    n_seq = span_order.shape[0]
+    n_tp = MODEL_WIDTH // width
+    me = lax.axis_index("seq")
+    slab = w_query.shape[0]
+    kv_heads = key_value_weight.shape[2] // HEAD_SIZE
+    share = n_seq // kv_heads
+    pieces = jnp.concatenate(
+        [
+            w_query.reshape(slab, n_seq, 1, HEAD_SIZE),
+            jnp.repeat(
+                key_value_weight.reshape(slab, 2, kv_heads, HEAD_SIZE).transpose(0, 2, 1, 3),
+                share,
+                axis=1,
+            ),
+        ],
+        axis=2,
+    ).transpose(1, 0, 2, 3).reshape(n_seq, slab, 3 * HEAD_SIZE)
+    weights = lax.all_to_all(pieces, "seq", split_axis=0, concat_axis=0, tiled=True)
+    weights = weights.reshape(n_tp, width, 3 * HEAD_SIZE)
+    local = hidden_in.astype(jnp.float32)
+    meansq = lax.psum(jnp.sum(local * local, axis=1, keepdims=True), "tp") / MODEL_WIDTH
+    normed_in = (
+        local * lax.rsqrt(meansq + eps) * norm_gain.astype(jnp.float32)[None, :]
+    ).astype(jnp.bfloat16)
+    everyone = lax.all_gather(normed_in, ("seq", "tp")).reshape(n_seq, n_tp, tok_rows, width)
+    tokens = n_seq * tok_rows
+    proj = jnp.einsum("stpr,trc->spc", everyone, weights, preferred_element_type=jnp.float32)
+    proj = proj.reshape(tokens, 3 * HEAD_SIZE)
+    bias_q = lax.dynamic_slice_in_dim(bias_query, me * HEAD_SIZE, HEAD_SIZE)
+    bias_pair = lax.dynamic_slice_in_dim(bias_kv, me // share * HEAD_SIZE, HEAD_SIZE, 1)
+    bias = jnp.concatenate([bias_q, bias_pair[0], bias_pair[1]]).astype(jnp.float32)
+    proj = proj + bias[None, :]
+    positions, cosine, sine = rope_tables(span_order, tok_rows)
+
+    def rotated(field):
+        return (field * cosine + jnp.roll(field, HEAD_SIZE // 2, axis=1) * sine).astype(jnp.bfloat16)
+
+    queries = rotated(proj[:, :HEAD_SIZE])
+    keys = rotated(proj[:, HEAD_SIZE : 2 * HEAD_SIZE])
+    values = proj[:, 2 * HEAD_SIZE :].astype(jnp.bfloat16)
+    attended = attention(queries, keys, values, positions)
+    heads = lax.all_gather(attended, "seq")
+    columns = w_out.shape[1]
+    partial_out = jnp.einsum(
+        "htd,hdc->tc",
+        heads,
+        w_out.reshape(n_seq, HEAD_SIZE, columns),
+        preferred_element_type=jnp.float32,
+    ).astype(jnp.bfloat16)
+    blocks = lax.all_to_all(
+        partial_out.reshape(n_seq, tok_rows, columns), "seq", split_axis=0, concat_axis=0, tiled=True
+    )
+    blocks = blocks.reshape(n_tp, n_seq // n_tp, tok_rows, columns)
+    terms = lax.all_to_all(blocks, "tp", split_axis=0, concat_axis=0, tiled=True)
+    mixed = jnp.sum(terms.astype(jnp.float32), axis=0).transpose(1, 0, 2).reshape(tok_rows, width)
+    attn_out = mixed.astype(jnp.bfloat16)
+    stream = local + mixed
+    post_sq = lax.psum(jnp.sum(stream * stream, axis=1), "tp")
+    normed = (
+        stream
+        * lax.rsqrt(post_sq / MODEL_WIDTH + eps)[:, None]
+        * post_gain.astype(jnp.float32)[None, :]
+    ).astype(jnp.bfloat16)
+    return (attn_out, normed)
+
+
+def per_device(*args):
+    hidden_in, span_order, w_query, kv_weight = args[0], args[1], args[3], args[5]
+    n_seq = span_order.shape[0]
+    n_tp = MODEL_WIDTH // hidden_in.shape[1]
+    heads = w_query.shape[1] // HEAD_SIZE
+    kv_heads = kv_weight.shape[2] // HEAD_SIZE
+    if heads == n_seq and n_seq == kv_heads * GROUP and n_seq % n_tp == 0:
+        return per_device_by_head(*args)
+    return per_device_by_span(*args)
+
+
 def solution(mesh):
     placed = (
         P("seq", "tp"),

time: 500 us -> 451 us (0.902)
  waiting for transfers between devices: 399 us -> 255 us
  local copies, waits for them, and re-layouts: 16.8 us -> 84.9 us
  blocking collectives: 9.42 us -> 39.4 us
  matrix products: 33.5 us -> 17.8 us
  Pallas kernels: 0 us -> 11.5 us
  starting transfers between devices: 0.46 us -> 9.8 us
  loops' own time: 5.47 us -> 0 us
    all_gather x6 -> x2, waiting for transfers between devices: 376 us -> 146 us  [the longest x1 73.1 us: per_device_by_head(): heads = lax.all_gather(attended, 'seq')]
    all_to_all x0 -> x2, waiting for transfers between devices: none -> 108 us  [the longest x1 94 us: per_device_by_head(): lax.all_to_all(pieces, 'seq', split_axis=0, concat_axis=0, tiled=True)]
    reshape x0 -> x3, local copies, waits for them, and re-layouts: none -> 68.6 us  [the longest x2 68.3 us: per_device_by_head(): lax.all_gather(normed_in, ('seq', 'tp'))]
    all_to_all x0 -> x1, blocking collectives: none -> 29.6 us  [per_device_by_head(): lax.all_to_all(partial_out.reshape(n_seq, tok_rows, columns), 'seq', spli...]
    reduce_scatter x1 -> x0, waiting for transfers between devices: 21.5 us -> none  [per_device(): lax.psum_scatter(partial_out.astype(jnp.bfloat16), 'tp', scatter_dimensio...]
    dot_general x11 -> x2, matrix products: 33.5 us -> 17.8 us  [the longest x1 13 us: per_device_by_head(): jnp.einsum('stpr,trc->spc', everyone, weights, preferred_element_type=jnp...]
    pallas_call x0 -> x1, Pallas kernels: none -> 11.5 us  [attention(): pl.pallas_call(attention_kernel, grid=(count // block,), in_specs=[rows,...]
    all_to_all x0 -> x2, starting transfers between devices: none -> 9.73 us  [the longest x1 6.15 us: per_device_by_head(): lax.all_to_all(pieces, 'seq', split_axis=0, concat_axis=0, tiled=True)]
  transfers between devices with their start and end apart: 7 -> 4, of which waited for: 7 -> 4; matrix products, arithmetic and copies ran while one was open for 9% -> 4% of each run, Pallas kernels for 0% -> 0%
where the time goes in v1:
time: 451 us; the launch traced here: 446 us
  waiting for transfers between devices  255 us (57%)
  local copies, waits for them, and re-layouts  84.9 us (19%)
  blocking collectives  39.4 us (9%)
  matrix products  17.8 us (4%)
  between operations  14.2 us (3%)
  other arithmetic  13.7 us (3%)
  Pallas kernels  11.5 us (3%)
  starting transfers between devices  9.8 us (2%)
    all_to_all x1, waiting for transfers between devices, per_device_by_head(): lax.all_to_all(pieces, 'seq', split_axis=0, concat_axis=0, tiled=True)  94 us
    all_gather x1, waiting for transfers between devices, per_device_by_head(): heads = lax.all_gather(attended, 'seq')  73.1 us
    all_gather x1, waiting for transfers between devices, per_device_by_head(): lax.all_gather(normed_in, ('seq', 'tp'))  73.1 us
    reshape x2, local copies, waits for them, and re-layouts, per_device_by_head(): lax.all_gather(normed_in, ('seq', 'tp'))  68.3 us
    all_to_all x1, blocking collectives, per_device_by_head(): lax.all_to_all(partial_out.reshape(n_seq, tok_rows, columns), 'seq', spli...  29.6 us
    all_to_all x1, waiting for transfers between devices, per_device_by_head(): lax.all_to_all(blocks, 'tp', split_axis=0, concat_axis=0, tiled=True)  14.4 us
    dot_general x1, matrix products, per_device_by_head(): jnp.einsum('stpr,trc->spc', everyone, weights, preferred_element_type=jnp...  13 us
    pallas_call x1, Pallas kernels, attention(): pl.pallas_call(attention_kernel, grid=(count // block,), in_specs=[rows,...  11.5 us
  transfers between devices with their start and end apart: 4, of which 4 were waited for; matrix products, arithmetic and copies ran while one was open for 4% of the time, Pallas kernels for 0%

profile of v1, /device:TPU:26, one launch (start us, length us, event | category | flops | bytes accessed | tf_op | source)
XLA Modules:
  0.0 446.0 jit_solution(15860336972925976417)
XLA Ops:
  7.2 0.0 copy-start
  7.2 0.0 all-gather.5.cloned.1.call-start
  7.2 1.4 copy.29
  8.7 0.7 convert_element_type.49
  9.4 0.3 fusion.1
  9.7 4.9 %psum.14 = f32[128,1]{0,1:T(1,128)S(1)} all-reduce(f32[128,1]{0,1:T(1,128)S(1)} %bitcast.57), channel_id=1, replica_groups=mesh['seq'=16,'tp'=2] {'tp'}, use_global_device_ids=true, to_apply=%region_1.0 | all-reduce | flops 128 | bytes 1024 | tf_op jit(solution)/shard_map/psum | solution.py:250
  14.6 1.1 fusion.3
  15.7 0.0 all-gather.5.cloned.1.call-update
  15.8 0.3 reshape.126
  16.1 0.3 copy.32
  16.4 1.5 copy.31
  17.9 0.2 broadcast_in_dim.5
  18.2 2.0 pad_maximum_fusion
  20.1 6.1 %all-to-all-start = ((bf16[16,256,384]{1,2,0:T(8,128)(2,1)}), bf16[16,256,384]{1,2,0:T(8,128)(2,1)}, u32[]{:S(2)}, u32[]{:S(2)}) async-start(bf16[16,256,384]{1,2,0:T(8,128)(2,1)} %bitcast.47), calls=%async_computation | async-start | bytes 6291456 | tf_op jit(solution)/shard_map/all_to_all | solution.py:247
  26.3 0.0 all-gather.7.cloned.1.call-start
  26.4 0.1 iota_add_fusion
  26.4 1.4 copy.36.qpos_ref
  27.9 0.8 dynamic_slice.6
  28.6 0.7 constant_dynamic-slice_fusion
  29.3 5.6 %fusion.8 = (f32[2048,64]{1,0:T(8,128)S(1)}, f32[2048,64]{1,0:T(8,128)}, f32[2048,64]{1,0:T(8,128)}) fusion(f32[64]{0:T(128)S(1)} %multiply_exponential_fusion, f32[2048]{0:T(1024)S(1)} %get-tuple-element.14), kind=kLoop, calls=%fused_computation.27 | loop fusion | flops 262144 | bytes 1581312 | tf_op jit(solution)/shard_map/neg | solution.py:173
  34.9 94.0 %all-to-all-done = bf16[16,256,384]{1,2,0:T(8,128)(2,1)} async-done(((bf16[16,256,384]{1,2,0:T(8,128)(2,1)}), bf16[16,256,384]{1,2,0:T(8,128)(2,1)}, u32[]{:S(2)}, u32[]{:S(2)}) %all-to-all-start) | async-done | bytes 3145760 | tf_op jit(solution)/shard_map/all_to_all | solution.py:247
  128.9 4.9 %copy.33 = bf16[16,256,384]{2,1,0:T(8,128)(2,1)} copy(bf16[16,256,384]{1,2,0:T(8,128)(2,1)} %all-to-all-done) | data formatting | bytes 6291456 | tf_op jit(solution)/shard_map/all_to_all | solution.py:247
  133.7 73.1 %all-gather.5.cloned.1.call-done = bf16[4096,2048]{0,1:T(8,128)(2,1)} async-done(((bf16[128,2048]{0,1:T(8,128)(2,1)}), bf16[4096,2048]{0,1:T(8,128)(2,1)}) %all-gather.5.cloned.1.call-update) | async-done | bytes 16777232 | tf_op jit(solution)/shard_map/all_gather | solution.py:254
  206.8 27.4 %reshape.124 = bf16[16,2,128,2048]{2,1,0,3:T(2,128)(2,1)} reshape(bf16[4096,2048]{0,1:T(8,128)(2,1)} %all-gather.5.cloned.1.call-done) | data formatting | bytes 33554432 | tf_op jit(solution)/shard_map/reshape | solution.py:254
  234.2 40.9 %copy.30 = bf16[16,2,128,2048]{3,2,0,1:T(8,128)(2,1)} copy(bf16[16,2,128,2048]{2,1,0,3:T(2,128)(2,1)} %reshape.124) | data formatting | bytes 33554432 | tf_op jit(solution)/shard_map/reshape | solution.py:254
  275.1 13.0 %bitcast_add_fusion = f32[2048,384]{1,0:T(8,128)S(1)} fusion(bf16[2048,2048,2]{1,0,2:T(8,128)(2,1)} %bitcast.46, bf16[2,2048,384]{2,1,0:T(8,128)(2,1)} %bitcast.52, f32[384]{0:T(512)S(1)} %maximum_convert_fusion), kind=kOutput, calls=%fused_computation.1 | convolution fusion | flops 6443237376 | bytes 23070208 | tf_op jit(solution)/shard_map/stpr,trc->spc/dot_general | solution.py:256
  288.1 0.0 copy-start.1
  288.1 0.0 copy-start.2
  288.1 0.7 fusion.9
  288.8 0.8 slice.63.v_ref
  289.6 0.0 copy-done.2
  289.6 2.1 fusion.5
  291.8 11.5 %attention.1 = bf16[2048,128]{1,0:T(8,128)(2,1)} custom-call(bf16[2048,128]{1,0:T(8,128)(2,1)} %get-tuple-element.5.q_ref, bf16[2048,128]{1,0:T(8,128)(2,1)} %get-tuple-element.4.k_ref, bf16[2048,128]{1,0:T(8,128)(2,1)} %slice.63.v_ref, s32[2048,1]{1,0:T(8,128)} %copy.36.qpos_ref, s32[1,2048]{1,0:T(1,128)} %bitcast.56), custom_call_target="tpu_custom_call" | custom-call | flops 2147483648 | bytes 2097152 | tf_op jit(solution)/shard_map/attention/pallas_call | solution.py:197
  303.3 0.0 all-gather.7.cloned.1.call-update
  303.3 73.1 %all-gather.7.cloned.1.call-done = bf16[32768,128]{1,0:T(8,128)(2,1)} async-done(((bf16[2048,128]{1,0:T(8,128)(2,1)}), bf16[32768,128]{1,0:T(8,128)(2,1)}) %all-gather.7.cloned.1.call-update) | async-done | bytes 8388624 | tf_op jit(solution)/shard_map/all_gather | solution.py:271
  376.4 4.8 %fusion = bf16[2048,256]{1,0:T(8,128)(2,1)S(1)} fusion(bf16[16,2048,128]{2,1,0:T(8,128)(2,1)} %bitcast.58, bf16[16,128,256]{2,1,0:T(8,128)(2,1)S(1)} %bitcast.45), kind=kOutput, calls=%fused_computation.3 | convolution fusion | flops 2148007936 | bytes 10485760 | tf_op jit(solution)/shard_map/htd,hdc->tc/dot_general | solution.py:273
  381.2 0.0 copy-start.5
  381.2 29.6 %all_to_all.15 = bf16[16,128,256]{2,1,0:T(8,128)(2,1)} all-to-all(bf16[16,128,256]{2,1,0:T(8,128)(2,1)S(1)} %bitcast.54), channel_id=1, replica_groups=mesh['seq'=16,'tp'=2] {'seq'}, dimensions={0} | all-to-all | bytes 2097152 | tf_op jit(solution)/shard_map/all_to_all | solution.py:279
  410.9 3.6 all-to-all-start.2
  414.5 14.4 %all-to-all-done.2 = bf16[2,8,128,256]{3,2,1,0:T(8,128)(2,1)S(1)} async-done(((bf16[2,8,128,256]{3,2,1,0:T(8,128)(2,1)}), bf16[2,8,128,256]{3,2,1,0:T(8,128)(2,1)S(1)}, u32[]{:S(2)}, u32[]{:S(2)}) %all-to-all-start.2) | async-done | bytes 1048608 | tf_op jit(solution)/shard_map/all_to_all | solution.py:283
  428.9 1.1 convert_reduce_fusion
  430.0 1.5 copy.37
  431.5 0.1 bitcast_convert_fusion
  431.6 0.3 multiply_reduce_fusion
  431.9 1.0 copy.38
  432.9 4.9 %psum.15 = f32[128]{0:T(128)S(1)} all-reduce(f32[128]{0:T(128)S(1)} %multiply_reduce_fusion), channel_id=1, replica_groups=mesh['seq'=16,'tp'=2] {'tp'}, use_global_device_ids=true, to_apply=%region_4.5 | all-reduce | flops 128 | bytes 1024 | tf_op jit(solution)/shard_map/psum | solution.py:287
  437.8 0.3 multiply_convert_fusion
  438.2 1.0 copy.39
  (16 shorter events, 0.1 us)
Async XLA Ops:
  7.2 369.2 %copy-start = (bf16[2048,256]{1,0:T(8,128)(2,1)S(1)}, bf16[2048,256]{1,0:T(8,128)(2,1)}, u32[]{:S(2)}) copy-start(bf16[2048,256]{1,0:T(8,128)(2,1)} %param.16) | copy-start | bytes 3145732
  7.2 8.6 %copy-start.3 = (bf16[256,2,512]{2,1,0:T(2,128)(2,1)S(1)}, bf16[256,2,512]{2,1,0:T(2,128)(2,1)}, u32[]{:S(2)}) copy-start(bf16[256,2,512]{2,1,0:T(2,128)(2,1)} %param.14) | copy-start | bytes 1572868
  7.2 199.6 %all-gather.5.cloned.1.call-start = ((), (), s32[]{:S(2)}) async-start(), calls=%async_computation.3 | async-start | bytes 17301504 | tf_op jit(solution)/shard_map/all_gather | solution.py:254
  20.1 6.2 %copy-start.6 = (s32[16]{0:T(128)S(1)}, s32[16]{0:T(128)}, u32[]{:S(2)}) copy-start(s32[16]{0:T(128)} %param.10) | copy-start | bytes 196
  20.1 108.7 %all-to-all-start = ((bf16[16,256,384]{1,2,0:T(8,128)(2,1)}), bf16[16,256,384]{1,2,0:T(8,128)(2,1)}, u32[]{:S(2)}, u32[]{:S(2)}) async-start(bf16[16,256,384]{1,2,0:T(8,128)(2,1)} %bitcast.47), calls=%async_computation | async-start | bytes 6291456 | tf_op jit(solution)/shard_map/all_to_all | solution.py:247
  26.3 350.1 %all-gather.7.cloned.1.call-start = ((), (), s32[]{:S(2)}) async-start(), calls=%async_computation.4 | async-start | bytes 8912896 | tf_op jit(solution)/shard_map/all_gather | solution.py:271
  26.4 107.3 %copy-start.4 = (s32[16,128]{1,0:T(8,128)}, s32[16,128]{1,0:T(8,128)S(1)}, u32[]{:S(2)}) copy-start(s32[16,128]{1,0:T(8,128)S(1)} %get-tuple-element.13) | copy-start | bytes 24580
  288.1 1.5 copy-start.1
  288.1 1.5 copy-start.2
  381.2 33.2 %copy-start.5 = (bf16[2048]{0:T(1024)(128)(2,1)S(1)}, bf16[2048]{0:T(1024)(128)(2,1)}, u32[]{:S(2)}) copy-start(bf16[2048]{0:T(1024)(128)(2,1)} %param.17) | copy-start | bytes 12292
  410.9 18.0 %all-to-all-start.2 = ((bf16[2,8,128,256]{3,2,1,0:T(8,128)(2,1)}), bf16[2,8,128,256]{3,2,1,0:T(8,128)(2,1)S(1)}, u32[]{:S(2)}, u32[]{:S(2)}) async-start(bf16[2,8,128,256]{3,2,1,0:T(8,128)(2,1)} %bitcast.49), calls=%async_computation.2 | async-start | bytes 2097152 | tf_op jit(solution)/shard_map/all_to_all | solution.py:283
Sparse Core Ops, SparseCore 0:
  15.9 190.9 all-gather.4
  303.4 72.9 all-gather.6

commit v2 on v1

--- a/solution.py
+++ b/solution.py
@@ -215,6 +215,287 @@
     )(queries, keys, values, positions[:, None], positions[None, :])
 
 
+MESH = pl.DeviceIdType.MESH
+CORES = 2
+PLANE = 4
+
+
+class Traffic:
+    def __init__(self, send_sem, peer):
+        self.send_sem, self.peer, self.started = send_sem, peer, []
+
+    def send(self, source, landing, arrival, target):
+        copy = pltpu.make_async_remote_copy(
+            src_ref=source,
+            dst_ref=landing,
+            send_sem=self.send_sem.at[len(self.started)],
+            recv_sem=arrival,
+            device_id=target,
+            device_id_type=MESH,
+        )
+        copy.start()
+        self.started.append(copy)
+
+    def arrive(self, landing, arrival):
+        pltpu.make_async_remote_copy(
+            src_ref=landing,
+            dst_ref=landing,
+            send_sem=self.send_sem.at[0],
+            recv_sem=arrival,
+            device_id=self.peer,
+            device_id_type=MESH,
+        ).wait_recv()
+
+    def finish(self):
+        for copy in self.started:
+            copy.wait_send()
+
+
+def place(n_seq):
+    s, t = lax.axis_index("seq"), lax.axis_index("tp")
+    return s, t, s // PLANE, s % PLANE // CORES, s % CORES
+
+
+def at(z, x, c):
+    return z * PLANE + x * CORES + c
+
+
+def exchange_kernel(
+    n_seq, chunk, q_in, kv_in, rows_out, q_out, kv_out, local_sem, send_sem, rows_sem, q_sem, kv_sem
+):
+    s, t, z, x, c = place(n_seq)
+    depth = n_seq // PLANE
+    offset = s % PLANE
+    sibling, across = (at(z, x, 1 - c), t), (at(z, 1 - x, c), t)
+    other = (s, 1 - t)
+    go = Traffic(send_sem, sibling)
+    stay = [
+        pltpu.make_async_copy(chunk, rows_out.at[s, t], local_sem.at[0]),
+        pltpu.make_async_copy(q_in.at[s], q_out.at[s], local_sem.at[1]),
+        pltpu.make_async_copy(kv_in.at[z], kv_out.at[s], local_sem.at[2]),
+    ]
+    for copy in stay:
+        copy.start()
+
+    def pass_on(source, owner, part, targets):
+        for target in targets:
+            go.send(source, rows_out.at[owner, part], rows_sem.at[owner, part], target)
+
+    def await_rows(owner, part):
+        go.arrive(rows_out.at[owner, part], rows_sem.at[owner, part])
+
+    far = [lax.rem(z + d, depth) for d in range(1, depth)]
+    near = [lax.rem(z - d + depth, depth) for d in range(depth)]
+    pass_on(chunk, s, t, [other, across])
+    pass_on(chunk, s, t, [(at(zt, x, c), t) for zt in far])
+    pass_on(chunk, s, t, [sibling])
+    for zt in far:
+        target = at(zt, x, c)
+        go.send(kv_in.at[zt], kv_out.at[s], kv_sem.at[s], (target, t))
+    mates = [lax.rem(offset + r, PLANE) for r in range(1, PLANE)]
+    for mate in mates:
+        go.send(kv_in.at[z], kv_out.at[s], kv_sem.at[s], (z * PLANE + mate, t))
+    for d in range(1, n_seq):
+        target = lax.rem(s + d, n_seq)
+        go.send(q_in.at[target], q_out.at[s], q_sem.at[s], (target, t))
+    for zs in near[1:]:
+        owner = at(zs, x, c)
+        await_rows(owner, t)
+        pass_on(rows_out.at[owner, t], owner, t, [other, across, sibling])
+    for zs in near:
+        owner = at(zs, 1 - x, c)
+        await_rows(owner, t)
+        pass_on(rows_out.at[owner, t], owner, t, [other, sibling])
+    for zs in near[1:]:
+        owner = at(zs, x, c)
+        go.arrive(kv_out.at[owner], kv_sem.at[owner])
+        for mate in mates:
+            go.send(kv_out.at[owner], kv_out.at[owner], kv_sem.at[owner], (z * PLANE + mate, t))
+    for xs in (x, 1 - x):
+        for zs in near:
+            owner = at(zs, xs, c)
+            await_rows(owner, 1 - t)
+            pass_on(rows_out.at[owner, 1 - t], owner, 1 - t, [sibling])
+    for part in (t, 1 - t):
+        for xs in (x, 1 - x):
+            for zs in near:
+                await_rows(at(zs, xs, 1 - c), part)
+    for d in range(1, n_seq):
+        owner = lax.rem(s - d + n_seq, n_seq)
+        go.arrive(q_out.at[owner], q_sem.at[owner])
+    for mate in mates:
+        for zs in near:
+            owner = zs * PLANE + mate
+            go.arrive(kv_out.at[owner], kv_sem.at[owner])
+    for copy in stay:
+        copy.wait()
+    go.finish()
+
+
+def exchange(chunk, q_pieces, kv_pieces, n_seq, n_tp):
+    vmem = pl.BlockSpec(memory_space=pltpu.VMEM)
+    hbm = pl.BlockSpec(memory_space=pl.ANY)
+    dma = pltpu.SemaphoreType.DMA
+    return pl.pallas_call(
+        lambda *refs: exchange_kernel(n_seq, *refs),
+        out_shape=(
+            jax.ShapeDtypeStruct((n_seq, n_tp) + chunk.shape, chunk.dtype),
+            jax.ShapeDtypeStruct(q_pieces.shape, q_pieces.dtype),
+            jax.ShapeDtypeStruct((n_seq,) + kv_pieces.shape[1:], kv_pieces.dtype),
+        ),
+        in_specs=[vmem] * 3,
+        out_specs=(hbm,) * 3,
+        scratch_shapes=[
+            dma((3,)),
+            dma((6 * n_seq,)),
+            dma((n_seq, n_tp)),
+            dma((n_seq,)),
+            dma((n_seq,)),
+        ],
+        compiler_params=pltpu.CompilerParams(has_side_effects=True),
+        name="exchange",
+    )(chunk, q_pieces, kv_pieces)
+
+
+def heads_kernel(n_seq, chunk, heads_out, local_sem, send_sem, heads_sem):
+    s, t, z, x, c = place(n_seq)
+    depth = n_seq // PLANE
+    sibling, across = (at(z, x, 1 - c), t), (at(z, 1 - x, c), t)
+    go = Traffic(send_sem, sibling)
+    stay = pltpu.make_async_copy(chunk, heads_out.at[s], local_sem.at[0])
+    stay.start()
+    near = [lax.rem(z - d + depth, depth) for d in range(depth)]
+    targets = [across] + [(at(lax.rem(z + d, depth), x, c), t) for d in range(1, depth)] + [sibling]
+    for target in targets:
+        go.send(chunk, heads_out.at[s], heads_sem.at[s], target)
+    for zs in near[1:]:
+        owner = at(zs, x, c)
+        go.arrive(heads_out.at[owner], heads_sem.at[owner])
+        for target in (across, sibling):
+            go.send(heads_out.at[owner], heads_out.at[owner], heads_sem.at[owner], target)
+    for zs in near:
+        owner = at(zs, 1 - x, c)
+        go.arrive(heads_out.at[owner], heads_sem.at[owner])
+        go.send(heads_out.at[owner], heads_out.at[owner], heads_sem.at[owner], sibling)
+    for xs in (x, 1 - x):
+        for zs in near:
+            owner = at(zs, xs, 1 - c)
+            go.arrive(heads_out.at[owner], heads_sem.at[owner])
+    stay.wait()
+    go.finish()
+
+
+def gather_heads(chunk, n_seq):
+    dma = pltpu.SemaphoreType.DMA
+    return pl.pallas_call(
+        lambda *refs: heads_kernel(n_seq, *refs),
+        out_shape=jax.ShapeDtypeStruct((n_seq,) + chunk.shape, chunk.dtype),
+        in_specs=[pl.BlockSpec(memory_space=pltpu.VMEM)],
+        out_specs=pl.BlockSpec(memory_space=pl.ANY),
+        scratch_shapes=[dma((1,)), dma((2 * n_seq,)), dma((n_seq,))],
+        compiler_params=pltpu.CompilerParams(has_side_effects=True),
+        name="gather_heads",
+    )(chunk)
+
+
+def return_kernel(n_seq, n_tp, blocks, terms, local_sem, send_sem, terms_sem):
+    s, t = lax.axis_index("seq"), lax.axis_index("tp")
+    half = n_seq // n_tp
+    goal, slot = s // half, s % half
+    go = Traffic(send_sem, (s, 1 - t))
+    for d in range(1, n_seq):
+        target = lax.rem(s + d, n_seq)
+        go.send(blocks.at[target], terms.at[t, slot], terms_sem.at[t, slot], (target, goal))
+
+    @pl.when(goal == t)
+    def _():
+        copy = pltpu.make_async_copy(blocks.at[s], terms.at[t, slot], local_sem.at[0])
+        copy.start()
+        copy.wait()
+
+    @pl.when(goal != t)
+    def _():
+        copy = pltpu.make_async_remote_copy(
+            src_ref=blocks.at[s],
+            dst_ref=terms.at[t, slot],
+            send_sem=send_sem.at[n_seq - 1],
+            recv_sem=terms_sem.at[t, slot],
+            device_id=(s, 1 - t),
+            device_id_type=MESH,
+        )
+        copy.start()
+        copy.wait_send()
+
+    for part in range(n_tp):
+        for k in range(half):
+            owner = t * half + k
+
+            @pl.when((owner != s) | (t != part))
+            def _():
+                go.arrive(terms.at[part, k], terms_sem.at[part, k])
+
+    go.finish()
+
+
+def return_blocks(blocks, n_seq, n_tp):
+    dma = pltpu.SemaphoreType.DMA
+    return pl.pallas_call(
+        lambda *refs: return_kernel(n_seq, n_tp, *refs),
+        out_shape=jax.ShapeDtypeStruct((n_tp, n_seq // n_tp) + blocks.shape[1:], blocks.dtype),
+        in_specs=[pl.BlockSpec(memory_space=pltpu.VMEM)],
+        out_specs=pl.BlockSpec(memory_space=pl.ANY),
+        scratch_shapes=[dma((1,)), dma((n_seq,)), dma((n_tp, n_seq // n_tp))],
+        compiler_params=pltpu.CompilerParams(has_side_effects=True),
+        name="return_blocks",
+    )(blocks)
+
+
+def project_kernel(rows, wq, wkv, bias, cosine, sine, q_ref, k_ref, v_ref):
+    spans, n_tp, span, width = rows.shape
+    first, pair = bias[:, :HEAD_SIZE], bias[:, HEAD_SIZE:]
+    query, both = first, pair
+    for part in range(n_tp):
+        piece = rows[:, part].reshape(spans * span, width)
+        query = query + jnp.dot(
+            piece, wq[pl.ds(part * width, width), :], preferred_element_type=jnp.float32
+        )
+        both = both + jnp.dot(
+            piece, wkv[pl.ds(part * width, width), :], preferred_element_type=jnp.float32
+        )
+
+    def rotated(field):
+        return (
+            field * cosine[...] + pltpu.roll(field, HEAD_SIZE // 2, 1) * sine[...]
+        ).astype(jnp.bfloat16)
+
+    q_ref[...] = rotated(query)
+    k_ref[...] = rotated(both[:, :HEAD_SIZE])
+    v_ref[...] = both[:, HEAD_SIZE:].astype(jnp.bfloat16)
+
+
+def project(rows, wq, wkv, bias, cosine, sine):
+    n_seq, n_tp, span, width = rows.shape
+    spans = math.gcd(n_seq, 4)
+    table = pl.BlockSpec((spans * span, HEAD_SIZE), lambda i: (i, 0))
+    whole = lambda a: pl.BlockSpec(a.shape, lambda i: (0, 0))
+    out = jax.ShapeDtypeStruct((n_seq * span, HEAD_SIZE), jnp.bfloat16)
+    return pl.pallas_call(
+        project_kernel,
+        grid=(n_seq // spans,),
+        in_specs=[
+            pl.BlockSpec((spans, n_tp, span, width), lambda i: (i, 0, 0, 0)),
+            whole(wq),
+            whole(wkv),
+            whole(bias),
+            table,
+            table,
+        ],
+        out_specs=(table,) * 3,
+        out_shape=(out,) * 3,
+        name="project",
+    )(rows, wq, wkv, bias, cosine, sine)
+
+
 def per_device_by_head(
     hidden_in,
     span_order,
@@ -233,42 +514,32 @@
     slab = w_query.shape[0]
     kv_heads = key_value_weight.shape[2] // HEAD_SIZE
     share = n_seq // kv_heads
-    pieces = jnp.concatenate(
-        [
-            w_query.reshape(slab, n_seq, 1, HEAD_SIZE),
-            jnp.repeat(
-                key_value_weight.reshape(slab, 2, kv_heads, HEAD_SIZE).transpose(0, 2, 1, 3),
-                share,
-                axis=1,
-            ),
-        ],
-        axis=2,
-    ).transpose(1, 0, 2, 3).reshape(n_seq, slab, 3 * HEAD_SIZE)
-    weights = lax.all_to_all(pieces, "seq", split_axis=0, concat_axis=0, tiled=True)
-    weights = weights.reshape(n_tp, width, 3 * HEAD_SIZE)
+    q_pieces = w_query.reshape(slab, n_seq, HEAD_SIZE).transpose(1, 0, 2)
+    kv_pieces = (
+        key_value_weight.reshape(slab, 2, kv_heads, HEAD_SIZE)
+        .transpose(2, 0, 1, 3)
+        .reshape(kv_heads, slab, 2 * HEAD_SIZE)
+    )
     local = hidden_in.astype(jnp.float32)
     meansq = lax.psum(jnp.sum(local * local, axis=1, keepdims=True), "tp") / MODEL_WIDTH
     normed_in = (
         local * lax.rsqrt(meansq + eps) * norm_gain.astype(jnp.float32)[None, :]
     ).astype(jnp.bfloat16)
-    everyone = lax.all_gather(normed_in, ("seq", "tp")).reshape(n_seq, n_tp, tok_rows, width)
-    tokens = n_seq * tok_rows
-    proj = jnp.einsum("stpr,trc->spc", everyone, weights, preferred_element_type=jnp.float32)
-    proj = proj.reshape(tokens, 3 * HEAD_SIZE)
+    rows, wq, wkv = exchange(normed_in, q_pieces, kv_pieces, n_seq, n_tp)
     bias_q = lax.dynamic_slice_in_dim(bias_query, me * HEAD_SIZE, HEAD_SIZE)
     bias_pair = lax.dynamic_slice_in_dim(bias_kv, me // share * HEAD_SIZE, HEAD_SIZE, 1)
     bias = jnp.concatenate([bias_q, bias_pair[0], bias_pair[1]]).astype(jnp.float32)
-    proj = proj + bias[None, :]
     positions, cosine, sine = rope_tables(span_order, tok_rows)
-
-    def rotated(field):
-        return (field * cosine + jnp.roll(field, HEAD_SIZE // 2, axis=1) * sine).astype(jnp.bfloat16)
-
-    queries = rotated(proj[:, :HEAD_SIZE])
-    keys = rotated(proj[:, HEAD_SIZE : 2 * HEAD_SIZE])
-    values = proj[:, 2 * HEAD_SIZE :].astype(jnp.bfloat16)
+    queries, keys, values = project(
+        rows,
+        wq.reshape(n_seq * slab, HEAD_SIZE),
+        wkv.reshape(n_seq * slab, 2 * HEAD_SIZE),
+        bias[None, :],
+        cosine,
+        sine,
+    )
     attended = attention(queries, keys, values, positions)
-    heads = lax.all_gather(attended, "seq")
+    heads = gather_heads(attended, n_seq)
     columns = w_out.shape[1]
     partial_out = jnp.einsum(
         "htd,hdc->tc",
@@ -276,11 +547,7 @@
         w_out.reshape(n_seq, HEAD_SIZE, columns),
         preferred_element_type=jnp.float32,
     ).astype(jnp.bfloat16)
-    blocks = lax.all_to_all(
-        partial_out.reshape(n_seq, tok_rows, columns), "seq", split_axis=0, concat_axis=0, tiled=True
-    )
-    blocks = blocks.reshape(n_tp, n_seq // n_tp, tok_rows, columns)
-    terms = lax.all_to_all(blocks, "tp", split_axis=0, concat_axis=0, tiled=True)
+    terms = return_blocks(partial_out.reshape(n_seq, tok_rows, columns), n_seq, n_tp)
     mixed = jnp.sum(terms.astype(jnp.float32), axis=0).transpose(1, 0, 2).reshape(tok_rows, width)
     attn_out = mixed.astype(jnp.bfloat16)
     stream = local + mixed
@@ -299,7 +566,7 @@
     n_tp = MODEL_WIDTH // hidden_in.shape[1]
     heads = w_query.shape[1] // HEAD_SIZE
     kv_heads = kv_weight.shape[2] // HEAD_SIZE
-    if heads == n_seq and n_seq == kv_heads * GROUP and n_seq % n_tp == 0:
+    if n_tp == 2 and heads == n_seq and n_seq == kv_heads * GROUP and GROUP == PLANE:
         return per_device_by_head(*args)
     return per_device_by_span(*args)
 

time: 451 us -> 318 us (0.71); the launches traced: 446 us -> 318 us
  Pallas kernels: 11.5 us -> 283 us
  waiting for transfers between devices: 255 us -> 0 us
  local copies, waits for them, and re-layouts: 84.9 us -> 7.36 us
  blocking collectives: 39.4 us -> 9.85 us
  between operations: 14.2 us -> 0.77 us
  matrix products: 17.8 us -> 5.89 us
  starting transfers between devices: 9.8 us -> 0 us
    pallas_call x0 -> x4, Pallas kernels: none -> 271 us  [the longest x1 144 us: exchange(): pl.pallas_call(lambda *refs: exchange_kernel(n_seq, *refs), out_shape=(ja...]
    all_gather x2 -> x0, waiting for transfers between devices: 146 us -> none  [the longest x1 73.1 us: per_device_by_head(): heads = lax.all_gather(attended, 'seq')]
    all_to_all x2 -> x0, waiting for transfers between devices: 108 us -> none  [the longest x1 94 us: per_device_by_head(): lax.all_to_all(pieces, 'seq', split_axis=0, concat_axis=0, tiled=True)]
    reshape x3, local copies, waits for them, and re-layouts: 68.6 us -> 2.57 us  [the longest x1 1.33 us: per_device_by_head(): q_pieces = w_query.reshape(slab, n_seq, HEAD_SIZE).transpose(1, 0, 2)]
    all_to_all x1 -> x0, blocking collectives: 29.6 us -> none  [per_device_by_head(): lax.all_to_all(partial_out.reshape(n_seq, tok_rows, columns), 'seq', spli...]
    dot_general x1 -> x0, matrix products: 13 us -> none  [per_device_by_head(): jnp.einsum('stpr,trc->spc', everyone, weights, preferred_element_type=jnp...]
    all_to_all x2 -> x0, starting transfers between devices: 9.73 us -> none  [the longest x1 6.15 us: per_device_by_head(): lax.all_to_all(pieces, 'seq', split_axis=0, concat_axis=0, tiled=True)]
    all_to_all x1 -> x0, local copies, waits for them, and re-layouts: 4.86 us -> none  [per_device_by_head(): lax.all_to_all(pieces, 'seq', split_axis=0, concat_axis=0, tiled=True)]
  transfers between devices with their start and end apart: 4 -> 0, of which waited for: 4 -> 0; matrix products, arithmetic and copies ran while one was open for 4% -> 0% of each run, Pallas kernels for 0% -> 0%
where the time goes in v2:
time: 318 us
  Pallas kernels  283 us (89%)
  other arithmetic  11.6 us (4%)
  blocking collectives  9.85 us (3%)
  local copies, waits for them, and re-layouts  7.36 us (2%)
  matrix products  5.89 us (2%)
    pallas_call x1, Pallas kernels, exchange(): pl.pallas_call(lambda *refs: exchange_kernel(n_seq, *refs), out_shape=(ja...  144 us
    pallas_call x1, Pallas kernels, gather_heads(): pl.pallas_call(lambda *refs: heads_kernel(n_seq, *refs), out_shape=jax.Sh...  78.5 us
    pallas_call x1, Pallas kernels, return_blocks(): pl.pallas_call(lambda *refs: return_kernel(n_seq, n_tp, *refs), out_shape...  35.2 us
    pallas_call x1, Pallas kernels, project(): pl.pallas_call(project_kernel, grid=(n_seq // spans,), in_specs=[pl.Block...  13.8 us
    pallas_call x1, Pallas kernels, attention(): pl.pallas_call(attention_kernel, grid=(count // block,), in_specs=[rows,...  11.5 us

profile of v2, /device:TPU:26, one launch (start us, length us, event | category | flops | bytes accessed | tf_op | source)
XLA Modules:
  0.0 318.1 jit_solution(11948840705090071051)
XLA Ops:
  0.6 0.0 copy-start
  0.6 0.0 copy-start.2
  0.7 0.0 copy-start.4
  0.7 0.0 copy-start.1
  0.7 0.8 constant_dynamic-slice_fusion
  1.5 0.8 dynamic-slice_bitcast_fusion
  2.3 0.5 maximum_convert_fusion.bias
  2.8 0.7 broadcast_multiply_fusion
  3.4 0.1 iota_add_fusion
  3.5 0.0 copy-start.3
  3.5 3.7 %fusion.4 = (f32[2048,64]{1,0:T(8,128)S(1)}, f32[2048,64]{1,0:T(8,128)S(1)}, f32[2048,64]{1,0:T(8,128)S(1)}) fusion(f32[64]{0:T(128)S(1)} %multiply_exponential_fusion, f32[2048]{0:T(1024)S(1)} %get-tuple-element.18), kind=kLoop, calls=%fused_computation.16 | loop fusion | flops 262144 | bytes 1581312 | tf_op jit(solution)/shard_map/neg | solution.py:173
  7.3 1.9 pad_maximum_fusion
  9.2 1.5 copy.16
  10.6 1.3 copy.17
  12.0 0.0 copy-done.2
  12.0 0.4 bitcast_bitcast_fusion
  12.3 1.1 reshape.134.refs_2_
  13.5 0.0 copy-done.4
  13.5 0.0 copy-done.1
  13.5 0.2 fusion.1
  13.7 4.9 %psum.14 = f32[128,1]{0,1:T(1,128)S(1)} all-reduce(f32[128,1]{0,1:T(1,128)S(1)} %bitcast.43), channel_id=1, replica_groups=mesh['seq'=16,'tp'=2] {'tp'}, use_global_device_ids=true, to_apply=%region_1.0 | all-reduce | flops 128 | bytes 1024 | tf_op jit(solution)/shard_map/psum | solution.py:524
  18.6 1.0 fusion.3.refs_0_
  19.6 143.5 %exchange.1 = (bf16[16,2,128,2048]{3,2,1,0:T(8,128)(2,1)}, bf16[16,256,128]{2,1,0:T(8,128)(2,1)}, bf16[16,256,256]{2,1,0:T(8,128)(2,1)}) custom-call(bf16[128,2048]{1,0:T(8,128)(2,1)} %fusion.3.refs_0_, bf16[16,256,128]{2,1,0:T(8,128)(2,1)} %bitcast.35, bf16[4,256,256]{2,1,0:T(8,128)(2,1)} %reshape.134.refs_2_), custom_call_target="tpu_custom_call" | custom-call | tf_op jit(solution)/shard_map/exchange/pallas_call | solution.py:339
  163.2 13.8 %project.1 = (bf16[2048,128]{1,0:T(8,128)(2,1)}, bf16[2048,128]{1,0:T(8,128)(2,1)}, bf16[2048,128]{1,0:T(8,128)(2,1)}) custom-call(bf16[16,2,128,2048]{3,2,1,0:T(8,128)(2,1)} %get-tuple-element.8.rows, bf16[4096,128]{1,0:T(8,128)(2,1)} %bitcast.39, bf16[4096,256]{1,0:T(8,128)(2,1)} %bitcast.38, f32[1,384]{1,0:T(1,128)} %maximum_convert_fusion.bias, ...), custom_call_target="tpu_custom_call" | custom-call | tf_op jit(solution)/shard_map/project/pallas_call | solution.py:482
  177.0 0.0 copy-done.3
  177.0 1.4 copy.19.qpos_ref
  178.3 11.5 %attention.1.refs_0_ = bf16[2048,128]{1,0:T(8,128)(2,1)} custom-call(bf16[2048,128]{1,0:T(8,128)(2,1)} %get-tuple-element.11.q_ref, bf16[2048,128]{1,0:T(8,128)(2,1)} %get-tuple-element.12.k_ref, bf16[2048,128]{1,0:T(8,128)(2,1)} %get-tuple-element.13.v_ref, s32[2048,1]{1,0:T(8,128)} %copy.19.qpos_ref, s32[1,2048]{1,0:T(1,128)} %bitcast.42), custom_call_target="tpu_custom_call" | custom-call | flops 2147483648 | bytes 2097152 | tf_op jit(solution)/shard_map/attention/pallas_call | solution.py:197
  189.9 78.5 %gather_heads.1 = bf16[16,2048,128]{2,1,0:T(8,128)(2,1)} custom-call(bf16[2048,128]{1,0:T(8,128)(2,1)} %attention.1.refs_0_), custom_call_target="tpu_custom_call" | custom-call | tf_op jit(solution)/shard_map/gather_heads/pallas_call | solution.py:390
  268.4 0.0 copy-done
  268.4 0.0 copy-start.5
  268.4 5.9 %fusion = bf16[2048,256]{1,0:T(8,128)(2,1)} fusion(bf16[16,2048,128]{2,1,0:T(8,128)(2,1)} %gather_heads.1, bf16[16,128,256]{2,1,0:T(8,128)(2,1)S(1)} %bitcast.31), kind=kOutput, calls=%fused_computation.1 | convolution fusion | flops 2148007936 | bytes 10485760 | tf_op jit(solution)/shard_map/htd,hdc->tc/dot_general | solution.py:544
  274.3 35.2 %return_blocks.1 = bf16[2,8,128,256]{3,2,1,0:T(8,128)(2,1)} custom-call(bf16[16,128,256]{2,1,0:T(8,128)(2,1)} %bitcast.40), custom_call_target="tpu_custom_call" | custom-call | tf_op jit(solution)/shard_map/return_blocks/pallas_call | solution.py:442
  309.5 1.5 convert_reduce_fusion
  311.0 0.1 copy.22
  311.1 0.2 multiply_reduce_fusion
  311.3 4.9 %psum.15 = f32[128]{0:T(128)S(1)} all-reduce(f32[128]{0:T(128)S(1)} %multiply_reduce_fusion), channel_id=1, replica_groups=mesh['seq'=16,'tp'=2] {'tp'}, use_global_device_ids=true, to_apply=%region_4.5 | all-reduce | flops 128 | bytes 1024 | tf_op jit(solution)/shard_map/psum | solution.py:554
  316.3 0.0 copy-done.5
  316.3 1.0 multiply_convert_fusion
  317.2 0.9 convert_element_type.52
  (6 shorter events, 0.0 us)
Async XLA Ops:
  0.6 267.8 %copy-start = (bf16[2048,256]{1,0:T(8,128)(2,1)S(1)}, bf16[2048,256]{1,0:T(8,128)(2,1)}, u32[]{:S(2)}) copy-start(bf16[2048,256]{1,0:T(8,128)(2,1)} %param.16) | copy-start | bytes 3145732
  0.6 11.3 %copy-start.2 = (bf16[256,2,512]{2,1,0:T(2,128)(2,1)S(1)}, bf16[256,2,512]{2,1,0:T(2,128)(2,1)}, u32[]{:S(2)}) copy-start(bf16[256,2,512]{2,1,0:T(2,128)(2,1)} %param.14) | copy-start | bytes 1572868
  0.7 12.8 %copy-start.4 = (bf16[2048]{0:T(1024)(128)(2,1)S(1)}, bf16[2048]{0:T(1024)(128)(2,1)}, u32[]{:S(2)}) copy-start(bf16[2048]{0:T(1024)(128)(2,1)} %param.11) | copy-start | bytes 12292
  0.7 12.8 %copy-start.1 = (bf16[128,2048]{1,0:T(8,128)(2,1)S(1)}, bf16[128,2048]{1,0:T(8,128)(2,1)}, u32[]{:S(2)}) copy-start(bf16[128,2048]{1,0:T(8,128)(2,1)} %param.9) | copy-start | bytes 1572868
  3.5 173.5 %copy-start.3 = (s32[16,128]{1,0:T(8,128)}, s32[16,128]{1,0:T(8,128)S(1)}, u32[]{:S(2)}) copy-start(s32[16,128]{1,0:T(8,128)S(1)} %get-tuple-element.17) | copy-start | bytes 24580
  268.4 47.8 %copy-start.5 = (bf16[2048]{0:T(1024)(128)(2,1)S(1)}, bf16[2048]{0:T(1024)(128)(2,1)}, u32[]{:S(2)}) copy-start(bf16[2048]{0:T(1024)(128)(2,1)} %param.17) | copy-start | bytes 12292

commit v3 on v2

--- a/solution.py
+++ b/solution.py
@@ -353,6 +353,7 @@
             dma((n_seq,)),
         ],
         compiler_params=pltpu.CompilerParams(has_side_effects=True),
+        cost_estimate=pl.CostEstimate(flops=0, bytes_accessed=16 * n_seq * n_tp * chunk.size, transcendentals=0),
         name="exchange",
     )(chunk, q_pieces, kv_pieces)
 
@@ -362,12 +363,14 @@
     depth = n_seq // PLANE
     sibling, across = (at(z, x, 1 - c), t), (at(z, 1 - x, c), t)
     go = Traffic(send_sem, sibling)
-    stay = pltpu.make_async_copy(chunk, heads_out.at[s], local_sem.at[0])
+    stay = pltpu.make_async_copy(chunk.at[z], heads_out.at[s], local_sem.at[0])
     stay.start()
     near = [lax.rem(z - d + depth, depth) for d in range(depth)]
-    targets = [across] + [(at(lax.rem(z + d, depth), x, c), t) for d in range(1, depth)] + [sibling]
-    for target in targets:
-        go.send(chunk, heads_out.at[s], heads_sem.at[s], target)
+    for d in range(1, depth):
+        zt = lax.rem(z + d, depth)
+        go.send(chunk.at[zt], heads_out.at[s], heads_sem.at[s], (at(zt, x, c), t))
+    for target in (across, sibling):
+        go.send(chunk.at[z], heads_out.at[s], heads_sem.at[s], target)
     for zs in near[1:]:
         owner = at(zs, x, c)
         go.arrive(heads_out.at[owner], heads_sem.at[owner])
@@ -389,7 +392,7 @@
     dma = pltpu.SemaphoreType.DMA
     return pl.pallas_call(
         lambda *refs: heads_kernel(n_seq, *refs),
-        out_shape=jax.ShapeDtypeStruct((n_seq,) + chunk.shape, chunk.dtype),
+        out_shape=jax.ShapeDtypeStruct((n_seq,) + chunk.shape[1:], chunk.dtype),
         in_specs=[pl.BlockSpec(memory_space=pltpu.VMEM)],
         out_specs=pl.BlockSpec(memory_space=pl.ANY),
         scratch_shapes=[dma((1,)), dma((2 * n_seq,)), dma((n_seq,))],
@@ -398,53 +401,64 @@
     )(chunk)
 
 
+def mix_kernel(depth, heads, *refs):
+    weights, out, flat = refs[:depth], refs[depth], refs[depth + 1]
+    z = lax.axis_index("seq") // PLANE
+    for head in range(heads.shape[0]):
+        flat[:, head * HEAD_SIZE : (head + 1) * HEAD_SIZE] = heads[head]
+    for d in range(depth):
+        out[lax.rem(z - d + depth, depth)] = jnp.dot(
+            flat[...], weights[d][...], preferred_element_type=jnp.float32
+        ).astype(jnp.bfloat16)
+
+
+def mix(heads, weights):
+    n_heads, rows, size = heads.shape
+    columns = weights[0].shape[1]
+    vmem = pl.BlockSpec(memory_space=pltpu.VMEM)
+    return pl.pallas_call(
+        lambda *refs: mix_kernel(len(weights), *refs),
+        out_shape=jax.ShapeDtypeStruct((len(weights), rows, columns), jnp.bfloat16),
+        in_specs=[vmem] * (1 + len(weights)),
+        out_specs=vmem,
+        scratch_shapes=[pltpu.VMEM((rows, n_heads * size), jnp.bfloat16)],
+        name="mix",
+    )(heads, *weights)
+
+
 def return_kernel(n_seq, n_tp, blocks, terms, local_sem, send_sem, terms_sem):
     s, t = lax.axis_index("seq"), lax.axis_index("tp")
-    half = n_seq // n_tp
-    goal, slot = s // half, s % half
+    z, offset = s // PLANE, s % PLANE
+    half = n_seq // PLANE // n_tp
     go = Traffic(send_sem, (s, 1 - t))
-    for d in range(1, n_seq):
-        target = lax.rem(s + d, n_seq)
-        go.send(blocks.at[target], terms.at[t, slot], terms_sem.at[t, slot], (target, goal))
-
-    @pl.when(goal == t)
-    def _():
-        copy = pltpu.make_async_copy(blocks.at[s], terms.at[t, slot], local_sem.at[0])
-        copy.start()
-        copy.wait()
-
-    @pl.when(goal != t)
-    def _():
-        copy = pltpu.make_async_remote_copy(
-            src_ref=blocks.at[s],
-            dst_ref=terms.at[t, slot],
-            send_sem=send_sem.at[n_seq - 1],
-            recv_sem=terms_sem.at[t, slot],
-            device_id=(s, 1 - t),
-            device_id_type=MESH,
+
+    def block(mate, goal):
+        return blocks.at[pl.ds(goal * half, half), mate]
+
+    pairs = [(r, q) for r in range(PLANE) for q in range(n_tp) if r or q]
+    for r, q in pairs:
+        mate, goal = lax.rem(offset + r, PLANE), lax.rem(t + q, n_tp)
+        go.send(
+            block(mate, goal), terms.at[t, offset], terms_sem.at[t, offset], (z * PLANE + mate, goal)
         )
-        copy.start()
-        copy.wait_send()
-
-    for part in range(n_tp):
-        for k in range(half):
-            owner = t * half + k
-
-            @pl.when((owner != s) | (t != part))
-            def _():
-                go.arrive(terms.at[part, k], terms_sem.at[part, k])
-
+    stay = pltpu.make_async_copy(block(offset, t), terms.at[t, offset], local_sem.at[0])
+    stay.start()
+    for r, q in pairs:
+        mate, part = lax.rem(offset + r, PLANE), lax.rem(t + q, n_tp)
+        go.arrive(terms.at[part, mate], terms_sem.at[part, mate])
+    stay.wait()
     go.finish()
 
 
 def return_blocks(blocks, n_seq, n_tp):
     dma = pltpu.SemaphoreType.DMA
+    depth, mates, rows, columns = blocks.shape
     return pl.pallas_call(
         lambda *refs: return_kernel(n_seq, n_tp, *refs),
-        out_shape=jax.ShapeDtypeStruct((n_tp, n_seq // n_tp) + blocks.shape[1:], blocks.dtype),
+        out_shape=jax.ShapeDtypeStruct((n_tp, mates, depth // n_tp, rows, columns), blocks.dtype),
         in_specs=[pl.BlockSpec(memory_space=pltpu.VMEM)],
         out_specs=pl.BlockSpec(memory_space=pl.ANY),
-        scratch_shapes=[dma((1,)), dma((n_seq,)), dma((n_tp, n_seq // n_tp))],
+        scratch_shapes=[dma((1,)), dma((n_tp * mates,)), dma((n_tp, mates))],
         compiler_params=pltpu.CompilerParams(has_side_effects=True),
         name="return_blocks",
     )(blocks)
@@ -492,6 +506,7 @@
         ],
         out_specs=(table,) * 3,
         out_shape=(out,) * 3,
+        cost_estimate=pl.CostEstimate(flops=6 * n_seq * n_tp * span * width * HEAD_SIZE, bytes_accessed=4 * rows.size, transcendentals=0),
         name="project",
     )(rows, wq, wkv, bias, cosine, sine)
 
@@ -514,6 +529,11 @@
     slab = w_query.shape[0]
     kv_heads = key_value_weight.shape[2] // HEAD_SIZE
     share = n_seq // kv_heads
+    depth = n_seq // PLANE
+    out_weights = [w_out] + [
+        lax.ppermute(w_out, "seq", [(i, (i + d * PLANE) % n_seq) for i in range(n_seq)])
+        for d in range(1, depth)
+    ]
     q_pieces = w_query.reshape(slab, n_seq, HEAD_SIZE).transpose(1, 0, 2)
     kv_pieces = (
         key_value_weight.reshape(slab, 2, kv_heads, HEAD_SIZE)
@@ -539,16 +559,11 @@
         sine,
     )
     attended = attention(queries, keys, values, positions)
-    heads = gather_heads(attended, n_seq)
+    heads = gather_heads(attended.reshape(depth, PLANE * tok_rows, HEAD_SIZE), n_seq)
+    partial_out = mix(heads, out_weights)
     columns = w_out.shape[1]
-    partial_out = jnp.einsum(
-        "htd,hdc->tc",
-        heads,
-        w_out.reshape(n_seq, HEAD_SIZE, columns),
-        preferred_element_type=jnp.float32,
-    ).astype(jnp.bfloat16)
-    terms = return_blocks(partial_out.reshape(n_seq, tok_rows, columns), n_seq, n_tp)
-    mixed = jnp.sum(terms.astype(jnp.float32), axis=0).transpose(1, 0, 2).reshape(tok_rows, width)
+    terms = return_blocks(partial_out.reshape(depth, PLANE, tok_rows, columns), n_seq, n_tp)
+    mixed = jnp.sum(terms.astype(jnp.float32), axis=0).transpose(2, 1, 0, 3).reshape(tok_rows, width)
     attn_out = mixed.astype(jnp.bfloat16)
     stream = local + mixed
     post_sq = lax.psum(jnp.sum(stream * stream, axis=1), "tp")
@@ -566,7 +581,7 @@
     n_tp = MODEL_WIDTH // hidden_in.shape[1]
     heads = w_query.shape[1] // HEAD_SIZE
     kv_heads = kv_weight.shape[2] // HEAD_SIZE
-    if n_tp == 2 and heads == n_seq and n_seq == kv_heads * GROUP and GROUP == PLANE:
+    if n_tp == 2 and heads == n_seq and n_seq == kv_heads * GROUP and GROUP == PLANE and n_seq % (PLANE * n_tp) == 0:
         return per_device_by_head(*args)
     return per_device_by_span(*args)
 

time: 318 us -> 321 us (level)
  matrix products: 5.89 us -> 0 us
    pallas_call x1, Pallas kernels: 144 us -> 204 us  [exchange(): pl.pallas_call(lambda *refs: exchange_kernel(n_seq, *refs), out_shape=(ja...]
    pallas_call x1, Pallas kernels: 78.5 us -> 27.4 us  [gather_heads(): pl.pallas_call(lambda *refs: heads_kernel(n_seq, *refs), out_shape=jax.Sh...]
    pallas_call x1, Pallas kernels: 35.2 us -> 18.9 us  [return_blocks(): pl.pallas_call(lambda *refs: return_kernel(n_seq, n_tp, *refs), out_shape...]
    pallas_call x0 -> x1, Pallas kernels: none -> 6.15 us  [mix(): pl.pallas_call(lambda *refs: mix_kernel(len(weights), *refs), out_shape=j...]
    dot_general x1 -> x0, matrix products: 5.89 us -> none  [per_device_by_head(): jnp.einsum('htd,hdc->tc', heads, w_out.reshape(n_seq, HEAD_SIZE, columns)...]
  transfers between devices with their start and end apart: 0 -> 3, of which waited for: 0 -> 0; matrix products, arithmetic and copies ran while one was open for 0% -> 6% of each run, Pallas kernels for 0% -> 81%
where the time goes in v3:
time: 321 us; the launch traced here: 318 us
  Pallas kernels  282 us (88%)
  other arithmetic  14.4 us (4%)
  blocking collectives  9.85 us (3%)
  local copies, waits for them, and re-layouts  8.41 us (3%)
    pallas_call x1, Pallas kernels, exchange(): pl.pallas_call(lambda *refs: exchange_kernel(n_seq, *refs), out_shape=(ja...  204 us
    pallas_call x1, Pallas kernels, gather_heads(): pl.pallas_call(lambda *refs: heads_kernel(n_seq, *refs), out_shape=jax.Sh...  27.4 us
    pallas_call x1, Pallas kernels, return_blocks(): pl.pallas_call(lambda *refs: return_kernel(n_seq, n_tp, *refs), out_shape...  18.9 us
    pallas_call x1, Pallas kernels, project(): pl.pallas_call(project_kernel, grid=(n_seq // spans,), in_specs=[pl.Block...  13.8 us
    pallas_call x1, Pallas kernels, attention(): pl.pallas_call(attention_kernel, grid=(count // block,), in_specs=[rows,...  11.5 us
  transfers between devices with their start and end apart: 3, of which 0 were waited for; matrix products, arithmetic and copies ran while one was open for 6% of the time, Pallas kernels for 81%

profile of v3, /device:TPU:26, one launch (start us, length us, event | category | flops | bytes accessed | tf_op | source)
XLA Modules:
  0.0 318.0 jit_solution(14348460491253620676)
XLA Ops:
  0.6 0.0 copy-start
  0.6 0.3 collective-permute-start
  0.9 1.7 collective-permute-start.1
  2.6 0.4 collective-permute-start.2
  3.1 0.7 constant_dynamic-slice_fusion
  3.7 0.7 broadcast_multiply_fusion
  4.4 0.1 iota_add_fusion
  4.5 0.0 copy-start.2
  4.5 1.5 copy.16
  6.0 0.0 copy-start.3
  6.0 0.0 copy-start.1
  6.0 1.4 copy.17
  7.4 0.0 copy-done
  7.4 0.4 bitcast_bitcast_fusion
  7.7 1.1 reshape.134.refs_2_
  8.9 0.0 copy-done.3
  8.9 0.0 copy-done.1
  8.9 0.2 fusion
  9.1 4.9 %psum.14 = f32[128,1]{0,1:T(1,128)S(1)} all-reduce(f32[128,1]{0,1:T(1,128)S(1)} %bitcast.30), channel_id=1, replica_groups=mesh['seq'=16,'tp'=2] {'tp'}, use_global_device_ids=true, to_apply=%region_1.0 | all-reduce | flops 128 | bytes 1024 | tf_op jit(solution)/shard_map/psum | solution.py:544
  14.0 0.0 copy-done.2
  14.0 1.4 copy.19.qpos_ref
  15.4 0.8 dynamic-slice_bitcast_fusion
  16.1 5.4 %fusion.3 = (f32[2048,64]{1,0:T(8,128)S(1)}, f32[2048,64]{1,0:T(8,128)S(1)}, f32[2048,64]{1,0:T(8,128)}) fusion(f32[64]{0:T(128)S(1)} %multiply_exponential_fusion, f32[2048]{0:T(1024)S(1)} %get-tuple-element.20), kind=kLoop, calls=%fused_computation.14 | loop fusion | flops 262144 | bytes 1581312 | tf_op jit(solution)/shard_map/neg | solution.py:173
  21.5 1.0 fusion.2.refs_0_
  22.5 0.6 maximum_convert_fusion.bias
  23.1 204.4 %exchange.1 = (bf16[16,2,128,2048]{3,2,1,0:T(8,128)(2,1)}, bf16[16,256,128]{2,1,0:T(8,128)(2,1)}, bf16[16,256,256]{2,1,0:T(8,128)(2,1)}) custom-call(bf16[128,2048]{1,0:T(8,128)(2,1)} %fusion.2.refs_0_, bf16[16,256,128]{2,1,0:T(8,128)(2,1)} %bitcast.24, bf16[4,256,256]{2,1,0:T(8,128)(2,1)} %reshape.134.refs_2_), custom_call_target="tpu_custom_call" | custom-call | bytes 134217728 | tf_op jit(solution)/shard_map/exchange/pallas_call | solution.py:339
  227.5 3.5 %pad_maximum_fusion = (f32[2048,128]{1,0:T(8,128)}, f32[2048,128]{1,0:T(8,128)}) fusion(f32[2048,64]{1,0:T(8,128)} %get-tuple-element.18, f32[2048,64]{1,0:T(8,128)S(1)} %get-tuple-element.17, f32[2048,64]{1,0:T(8,128)S(1)} %get-tuple-element.16), kind=kLoop, calls=%fused_computation.9 | loop fusion | flops 524288 | bytes 3670016 | tf_op jit(solution)/shard_map/concatenate | solution.py:172
  231.0 13.8 %project.1 = (bf16[2048,128]{1,0:T(8,128)(2,1)}, bf16[2048,128]{1,0:T(8,128)(2,1)}, bf16[2048,128]{1,0:T(8,128)(2,1)}) custom-call(bf16[16,2,128,2048]{3,2,1,0:T(8,128)(2,1)} %get-tuple-element.8.rows, bf16[4096,128]{1,0:T(8,128)(2,1)} %bitcast.32, bf16[4096,256]{1,0:T(8,128)(2,1)} %bitcast.31, f32[1,384]{1,0:T(1,128)} %maximum_convert_fusion.bias, ...), custom_call_target="tpu_custom_call" | custom-call | flops 6442450944 | bytes 33554432 | tf_op jit(solution)/shard_map/project/pallas_call | solution.py:496
  244.8 11.5 %attention.1 = bf16[2048,128]{1,0:T(8,128)(2,1)} custom-call(bf16[2048,128]{1,0:T(8,128)(2,1)} %get-tuple-element.11.q_ref, bf16[2048,128]{1,0:T(8,128)(2,1)} %get-tuple-element.12.k_ref, bf16[2048,128]{1,0:T(8,128)(2,1)} %get-tuple-element.13.v_ref, s32[2048,1]{1,0:T(8,128)} %copy.19.qpos_ref, s32[1,2048]{1,0:T(1,128)} %bitcast.29), custom_call_target="tpu_custom_call" | custom-call | flops 2147483648 | bytes 2097152 | tf_op jit(solution)/shard_map/attention/pallas_call | solution.py:197
  256.4 0.0 copy-start.4
  256.4 27.4 %gather_heads.1.refs_0_ = bf16[16,512,128]{2,1,0:T(8,128)(2,1)} custom-call(bf16[4,512,128]{2,1,0:T(8,128)(2,1)} %bitcast.27), custom_call_target="tpu_custom_call" | custom-call | tf_op jit(solution)/shard_map/gather_heads/pallas_call | solution.py:393
  283.8 0.0 copy-done.4
  283.8 0.0 collective-permute-done.refs_2_
  283.8 0.0 collective-permute-done.1.refs_3_
  283.8 0.0 collective-permute-done.2.refs_4_
  283.8 6.2 %mix.1 = bf16[4,512,256]{2,1,0:T(8,128)(2,1)} custom-call(bf16[16,512,128]{2,1,0:T(8,128)(2,1)} %gather_heads.1.refs_0_, bf16[2048,256]{1,0:T(8,128)(2,1)} %refs_1_.1, bf16[2048,256]{1,0:T(8,128)(2,1)} %collective-permute-done.refs_2_, bf16[2048,256]{1,0:T(8,128)(2,1)} %collective-permute-done.1.refs_3_, bf16[2048,256]{1,0:T(8,128)(2,1)} %collective-permute-done.2.refs_4_), custom_call_target="tpu_custom_call" | custom-call | tf_op jit(solution)/shard_map/mix/pallas_call | solution.py:419
  290.0 18.9 %return_blocks.1 = bf16[2,4,2,128,256]{4,3,2,1,0:T(8,128)(2,1)} custom-call(bf16[4,4,128,256]{3,2,1,0:T(8,128)(2,1)} %bitcast.23), custom_call_target="tpu_custom_call" | custom-call | tf_op jit(solution)/shard_map/return_blocks/pallas_call | solution.py:456
  308.9 1.5 convert_reduce_fusion
  310.4 0.7 copy.20
  311.1 0.5 reshape.139
  311.6 0.2 multiply_reduce_fusion
  311.8 4.9 %psum.15 = f32[128]{0:T(128)S(1)} all-reduce(f32[128]{0:T(128)S(1)} %multiply_reduce_fusion), channel_id=1, replica_groups=mesh['seq'=16,'tp'=2] {'tp'}, use_global_device_ids=true, to_apply=%region_4.5 | all-reduce | flops 128 | bytes 1024 | tf_op jit(solution)/shard_map/psum | solution.py:569
  316.8 1.2 multiply_convert_fusion
  (6 shorter events, 0.0 us)
Async XLA Ops:
  0.6 6.7 %copy-start = (bf16[256,2,512]{2,1,0:T(2,128)(2,1)S(1)}, bf16[256,2,512]{2,1,0:T(2,128)(2,1)}, u32[]{:S(2)}) copy-start(bf16[256,2,512]{2,1,0:T(2,128)(2,1)} %param.14) | copy-start | bytes 1572868
  0.6 283.2 %collective-permute-start = (bf16[2048,256]{1,0:T(8,128)(2,1)}, bf16[2048,256]{1,0:T(8,128)(2,1)}, u32[]{:S(2)}, u32[]{:S(2)}) collective-permute-start(bf16[2048,256]{1,0:T(8,128)(2,1)} %refs_1_.1), channel_id=1, source_target_pairs={{0,8},{2,10},{4,12},{6,14},{8,16},{10,18},{12,20},{14,22},{16,24},... | collective-permute-start | bytes 3145736 | tf_op jit(solution)/shard_map/ppermute | solution.py:534
  0.9 282.9 %collective-permute-start.1 = (bf16[2048,256]{1,0:T(8,128)(2,1)}, bf16[2048,256]{1,0:T(8,128)(2,1)}, u32[]{:S(2)}, u32[]{:S(2)}) collective-permute-start(bf16[2048,256]{1,0:T(8,128)(2,1)} %refs_1_.1), channel_id=1, source_target_pairs={{0,16},{2,18},{4,20},{6,22},{8,24},{10,26},{12,28},{14,30},{16,0},... | collective-permute-start | bytes 3145736 | tf_op jit(solution)/shard_map/ppermute | solution.py:534
  2.6 281.2 %collective-permute-start.2 = (bf16[2048,256]{1,0:T(8,128)(2,1)}, bf16[2048,256]{1,0:T(8,128)(2,1)}, u32[]{:S(2)}, u32[]{:S(2)}) collective-permute-start(bf16[2048,256]{1,0:T(8,128)(2,1)} %refs_1_.1), channel_id=1, source_target_pairs={{0,24},{2,26},{4,28},{6,30},{8,0},{10,2},{12,4},{14,6},{16,8},{18,... | collective-permute-start | bytes 3145736 | tf_op jit(solution)/shard_map/ppermute | solution.py:534
  4.5 9.5 %copy-start.2 = (s32[16,128]{1,0:T(8,128)}, s32[16,128]{1,0:T(8,128)S(1)}, u32[]{:S(2)}) copy-start(s32[16,128]{1,0:T(8,128)S(1)} %get-tuple-element.19) | copy-start | bytes 24580
  6.0 2.9 copy-start.3
  6.0 2.9 copy-start.1
  256.4 27.4 %copy-start.4 = (bf16[2048]{0:T(1024)(128)(2,1)S(1)}, bf16[2048]{0:T(1024)(128)(2,1)}, u32[]{:S(2)}) copy-start(bf16[2048]{0:T(1024)(128)(2,1)} %param.17) | copy-start | bytes 12292

commit v4 on v3

--- a/solution.py
+++ b/solution.py
@@ -529,11 +529,6 @@
     slab = w_query.shape[0]
     kv_heads = key_value_weight.shape[2] // HEAD_SIZE
     share = n_seq // kv_heads
-    depth = n_seq // PLANE
-    out_weights = [w_out] + [
-        lax.ppermute(w_out, "seq", [(i, (i + d * PLANE) % n_seq) for i in range(n_seq)])
-        for d in range(1, depth)
-    ]
     q_pieces = w_query.reshape(slab, n_seq, HEAD_SIZE).transpose(1, 0, 2)
     kv_pieces = (
         key_value_weight.reshape(slab, 2, kv_heads, HEAD_SIZE)
@@ -546,6 +541,12 @@
         local * lax.rsqrt(meansq + eps) * norm_gain.astype(jnp.float32)[None, :]
     ).astype(jnp.bfloat16)
     rows, wq, wkv = exchange(normed_in, q_pieces, kv_pieces, n_seq, n_tp)
+    rows, wq, wkv, w_out = lax.optimization_barrier((rows, wq, wkv, w_out))
+    depth = n_seq // PLANE
+    out_weights = [w_out] + [
+        lax.ppermute(w_out, "seq", [(i, (i + d * PLANE) % n_seq) for i in range(n_seq)])
+        for d in range(1, depth)
+    ]
     bias_q = lax.dynamic_slice_in_dim(bias_query, me * HEAD_SIZE, HEAD_SIZE)
     bias_pair = lax.dynamic_slice_in_dim(bias_kv, me // share * HEAD_SIZE, HEAD_SIZE, 1)
     bias = jnp.concatenate([bias_q, bias_pair[0], bias_pair[1]]).astype(jnp.float32)

time: 321 us -> 302 us (0.941)
  Pallas kernels: 282 us -> 266 us
  other arithmetic: 14.4 us -> 10.4 us
    pallas_call x1, Pallas kernels: 204 us -> 144 us  [exchange(): pl.pallas_call(lambda *refs: exchange_kernel(n_seq, *refs), out_shape=(ja...]
    pallas_call x1, Pallas kernels: 27.4 us -> 65.6 us  [gather_heads(): pl.pallas_call(lambda *refs: heads_kernel(n_seq, *refs), out_shape=jax.Sh...]
    pallas_call x1, Pallas kernels: 18.9 us -> 25.5 us  [return_blocks(): pl.pallas_call(lambda *refs: return_kernel(n_seq, n_tp, *refs), out_shape...]
  transfers between devices with their start and end apart: 3 -> 3, of which waited for: 0 -> 0; matrix products, arithmetic and copies ran while one was open for 6% -> 3% of each run, Pallas kernels for 81% -> 30%
where the time goes in v4:
time: 302 us; the launch traced here: 299 us
  Pallas kernels  266 us (88%)
  other arithmetic  10.4 us (3%)
  blocking collectives  9.98 us (3%)
  local copies, waits for them, and re-layouts  9.35 us (3%)
    pallas_call x1, Pallas kernels, exchange(): pl.pallas_call(lambda *refs: exchange_kernel(n_seq, *refs), out_shape=(ja...  144 us
    pallas_call x1, Pallas kernels, gather_heads(): pl.pallas_call(lambda *refs: heads_kernel(n_seq, *refs), out_shape=jax.Sh...  65.6 us
    pallas_call x1, Pallas kernels, return_blocks(): pl.pallas_call(lambda *refs: return_kernel(n_seq, n_tp, *refs), out_shape...  25.5 us
    pallas_call x1, Pallas kernels, project(): pl.pallas_call(project_kernel, grid=(n_seq // spans,), in_specs=[pl.Block...  13.8 us
    pallas_call x1, Pallas kernels, attention(): pl.pallas_call(attention_kernel, grid=(count // block,), in_specs=[rows,...  11.5 us
    pallas_call x1, Pallas kernels, mix(): pl.pallas_call(lambda *refs: mix_kernel(len(weights), *refs), out_shape=j...  6.15 us
  transfers between devices with their start and end apart: 3, of which 0 were waited for; matrix products, arithmetic and copies ran while one was open for 3% of the time, Pallas kernels for 30%

profile of v4, /device:TPU:26, one launch (start us, length us, event | category | flops | bytes accessed | tf_op | source)
XLA Modules:
  0.0 298.8 jit_solution(6170435474664284250)
XLA Ops:
  0.6 0.0 copy-start
  0.6 1.5 copy.16
  2.2 0.0 copy-start.5
  2.2 0.0 copy-start.1
  2.2 1.3 copy.17
  3.6 0.0 copy-done
  3.6 0.4 bitcast_bitcast_fusion
  3.9 1.1 reshape.134.refs_2_
  5.0 0.0 copy-done.5
  5.0 0.0 copy-start.2
  5.1 0.0 copy-start.7
  5.1 0.0 copy-done.1
  5.1 0.2 fusion
  5.3 5.1 %psum.14 = f32[128,1]{0,1:T(1,128)S(1)} all-reduce(f32[128,1]{0,1:T(1,128)S(1)} %bitcast.30), channel_id=1, replica_groups=mesh['seq'=16,'tp'=2] {'tp'}, use_global_device_ids=true, to_apply=%region_1.0 | all-reduce | flops 128 | bytes 1024 | tf_op jit(solution)/shard_map/psum | solution.py:539
  10.3 1.0 fusion.2.refs_0_
  11.3 143.5 %exchange.1 = (bf16[16,2,128,2048]{3,2,1,0:T(8,128)(2,1)}, bf16[16,256,128]{2,1,0:T(8,128)(2,1)}, bf16[16,256,256]{2,1,0:T(8,128)(2,1)}) custom-call(bf16[128,2048]{1,0:T(8,128)(2,1)} %fusion.2.refs_0_, bf16[16,256,128]{2,1,0:T(8,128)(2,1)} %bitcast.24, bf16[4,256,256]{2,1,0:T(8,128)(2,1)} %reshape.134.refs_2_), custom_call_target="tpu_custom_call" | custom-call | bytes 134217728 | tf_op jit(solution)/shard_map/exchange/pallas_call | solution.py:339
  154.9 0.0 copy-done.2
  154.9 0.1 collective-permute-start
  154.9 0.1 collective-permute-start.1
  155.0 1.9 collective-permute-start.2
  157.0 0.7 constant_dynamic-slice_fusion
  157.6 0.0 copy-done.7
  157.7 0.1 iota_add_fusion
  157.7 0.0 copy-start.4
  157.7 1.4 copy.19.qpos_ref
  159.1 0.8 dynamic-slice_bitcast_fusion
  159.8 3.7 %fusion.3 = (f32[2048,64]{1,0:T(8,128)S(1)}, f32[2048,64]{1,0:T(8,128)S(1)}, f32[2048,64]{1,0:T(8,128)S(1)}) fusion(f32[64]{0:T(128)S(1)} %multiply_exponential_fusion, f32[2048]{0:T(1024)S(1)} %get-tuple-element.28), kind=kLoop, calls=%fused_computation.14 | loop fusion | flops 262144 | bytes 1581312 | tf_op jit(solution)/shard_map/neg | solution.py:173
  163.6 0.0 copy-done.4
  163.6 0.5 maximum_convert_fusion.bias
  164.1 2.0 pad_maximum_fusion
  166.1 13.8 %project.1 = (bf16[2048,128]{1,0:T(8,128)(2,1)}, bf16[2048,128]{1,0:T(8,128)(2,1)}, bf16[2048,128]{1,0:T(8,128)(2,1)}) custom-call(bf16[16,2,128,2048]{3,2,1,0:T(8,128)(2,1)} %get-tuple-element.15.rows, bf16[4096,128]{1,0:T(8,128)(2,1)} %bitcast.32, bf16[4096,256]{1,0:T(8,128)(2,1)} %bitcast.31, f32[1,384]{1,0:T(1,128)} %maximum_convert_fusion.bias, ...), custom_call_target="tpu_custom_call" | custom-call | flops 6442450944 | bytes 33554432 | tf_op jit(solution)/shard_map/project/pallas_call | solution.py:496
  179.9 11.5 %attention.1 = bf16[2048,128]{1,0:T(8,128)(2,1)} custom-call(bf16[2048,128]{1,0:T(8,128)(2,1)} %get-tuple-element.18.q_ref, bf16[2048,128]{1,0:T(8,128)(2,1)} %get-tuple-element.19.k_ref, bf16[2048,128]{1,0:T(8,128)(2,1)} %get-tuple-element.20.v_ref, s32[2048,1]{1,0:T(8,128)} %copy.19.qpos_ref, s32[1,2048]{1,0:T(1,128)} %bitcast.29), custom_call_target="tpu_custom_call" | custom-call | flops 2147483648 | bytes 2097152 | tf_op jit(solution)/shard_map/attention/pallas_call | solution.py:197
  191.4 0.0 copy-start.6
  191.4 65.6 %gather_heads.1.refs_0_ = bf16[16,512,128]{2,1,0:T(8,128)(2,1)} custom-call(bf16[4,512,128]{2,1,0:T(8,128)(2,1)} %bitcast.27), custom_call_target="tpu_custom_call" | custom-call | tf_op jit(solution)/shard_map/gather_heads/pallas_call | solution.py:393
  257.0 0.0 copy-done.6
  257.0 0.0 collective-permute-done.refs_2_
  257.1 0.0 copy-start.3
  257.1 0.0 collective-permute-done.1.refs_3_
  257.1 0.0 collective-permute-done.2.refs_4_
  257.1 1.0 copy-done.3
  258.0 6.1 %mix.1 = bf16[4,512,256]{2,1,0:T(8,128)(2,1)} custom-call(bf16[16,512,128]{2,1,0:T(8,128)(2,1)} %gather_heads.1.refs_0_, bf16[2048,256]{1,0:T(8,128)(2,1)} %refs_1_, bf16[2048,256]{1,0:T(8,128)(2,1)} %copy-done.3, bf16[2048,256]{1,0:T(8,128)(2,1)} %collective-permute-done.1.refs_3_, bf16[2048,256]{1,0:T(8,128)(2,1)} %collective-permute-done.2.refs_4_), custom_call_target="tpu_custom_call" | custom-call | tf_op jit(solution)/shard_map/mix/pallas_call | solution.py:419
  264.2 25.5 %return_blocks.1 = bf16[2,4,2,128,256]{4,3,2,1,0:T(8,128)(2,1)} custom-call(bf16[4,4,128,256]{3,2,1,0:T(8,128)(2,1)} %bitcast.23), custom_call_target="tpu_custom_call" | custom-call | tf_op jit(solution)/shard_map/return_blocks/pallas_call | solution.py:456
  289.7 1.5 convert_reduce_fusion
  291.2 0.7 copy.20
  291.9 0.5 reshape.139
  292.5 0.2 multiply_reduce_fusion
  292.7 4.9 %psum.15 = f32[128]{0:T(128)S(1)} all-reduce(f32[128]{0:T(128)S(1)} %multiply_reduce_fusion), channel_id=1, replica_groups=mesh['seq'=16,'tp'=2] {'tp'}, use_global_device_ids=true, to_apply=%region_4.5 | all-reduce | flops 128 | bytes 1024 | tf_op jit(solution)/shard_map/psum | solution.py:570
  297.6 1.2 multiply_convert_fusion
  (7 shorter events, 0.0 us)
Async XLA Ops:
  0.6 2.9 copy-start
  2.2 2.9 copy-start.5
  2.2 2.9 copy-start.1
  5.0 149.8 %copy-start.2 = (bf16[2048,256]{1,0:T(8,128)(2,1)S(1)}, bf16[2048,256]{1,0:T(8,128)(2,1)}, u32[]{:S(2)}) copy-start(bf16[2048,256]{1,0:T(8,128)(2,1)} %refs_1_) | copy-start | bytes 3145732
  5.1 152.6 %copy-start.7 = (s32[16]{0:T(128)S(1)}, s32[16]{0:T(128)}, u32[]{:S(2)}) copy-start(s32[16]{0:T(128)} %param.10) | copy-start | bytes 196
  154.9 102.2 %collective-permute-start = (bf16[2048,256]{1,0:T(8,128)(2,1)S(1)}, bf16[2048,256]{1,0:T(8,128)(2,1)S(1)}, u32[]{:S(2)}, u32[]{:S(2)}) collective-permute-start(bf16[2048,256]{1,0:T(8,128)(2,1)S(1)} %copy-done.2), channel_id=1, source_target_pairs={{0,8},{2,10},{4,12},{6,14},{8,16},{10,18},{12,20},{14,22},{16,24},... | collective-permute-start | bytes 3145736 | tf_op jit(solution)/shard_map/ppermute | solution.py:547
  154.9 102.1 %collective-permute-start.1 = (bf16[2048,256]{1,0:T(8,128)(2,1)S(1)}, bf16[2048,256]{1,0:T(8,128)(2,1)}, u32[]{:S(2)}, u32[]{:S(2)}) collective-permute-start(bf16[2048,256]{1,0:T(8,128)(2,1)S(1)} %copy-done.2), channel_id=1, source_target_pairs={{0,16},{2,18},{4,20},{6,22},{8,24},{10,26},{12,28},{14,30},{16,0},... | collective-permute-start | bytes 3145736 | tf_op jit(solution)/shard_map/ppermute | solution.py:547
  155.0 102.1 %collective-permute-start.2 = (bf16[2048,256]{1,0:T(8,128)(2,1)S(1)}, bf16[2048,256]{1,0:T(8,128)(2,1)}, u32[]{:S(2)}, u32[]{:S(2)}) collective-permute-start(bf16[2048,256]{1,0:T(8,128)(2,1)S(1)} %copy-done.2), channel_id=1, source_target_pairs={{0,24},{2,26},{4,28},{6,30},{8,0},{10,2},{12,4},{14,6},{16,8},{18,... | collective-permute-start | bytes 3145736 | tf_op jit(solution)/shard_map/ppermute | solution.py:547
  157.7 5.8 %copy-start.4 = (s32[16,128]{1,0:T(8,128)}, s32[16,128]{1,0:T(8,128)S(1)}, u32[]{:S(2)}) copy-start(s32[16,128]{1,0:T(8,128)S(1)} %get-tuple-element.27) | copy-start | bytes 24580
  191.4 65.6 %copy-start.6 = (bf16[2048]{0:T(1024)(128)(2,1)S(1)}, bf16[2048]{0:T(1024)(128)(2,1)}, u32[]{:S(2)}) copy-start(bf16[2048]{0:T(1024)(128)(2,1)} %param.17) | copy-start | bytes 12292
  257.1 1.0 copy-start.3
